TPU v7x, 32 devices: a whole 2x2x4 slice. The times are simulated.
32 devices in a mesh: row: 8 (over z, x), col: 4 (over y, core).
Axes of the slice: x: 2, y: 2, z: 4, core: 2. Of those that a mesh axis runs over, the one named last changes fastest.
Arguments:
- tiles: bfloat16 [8, 4, 3, 256, 256], P('row', 'col'), as said below
- stack_index: int32 [8, 4, 3], P('row', 'col'), may hold values from 0 to 127, as said below
- block_mask: int32 [64, 64], replicated, may hold values from 0 to 1, as said below
Outputs:
- purified: bfloat16 [8, 4, 3, 256, 256], P('row', 'col')
Inputs may be any that keep to these rules, and one draw needn't show every extreme that they name: `block_mask`: the region of one device (8 x 16 blocks) holds at most 3 occupied blocks; some region holds exactly 3 in every draw. `stack_index`: block (a, b) of a device's region is numbered a * 16 + b. A device's 3 entries are distinct and include every occupied block of its region; a slot naming an unoccupied block holds a tile that P does not use. `tiles`: A slot's tile is P's block named by stack_index when that block is occupied.
All inputs are finite; a program needn't handle non-finite values.
Results may differ from a plain program's by a relative error of at most 0.0051.
Values may be sent and summed in bfloat16 or wider, within the bound.
A program may use at most 64 MiB of HBM per device.

v0:
```python
import jax
import jax.numpy as jnp
from jax import lax
from jax.sharding import PartitionSpec as P

NB = 64


def shortened(shard):

    def short(part):
        return part.astype(jnp.bfloat16) if part.dtype == jnp.float32 else part

    return jax.tree.map(short, shard)


def shifted(shard, axis, by):
    length = lax.axis_size(axis)
    return lax.ppermute(shard, axis, [(i, (i + by) % length) for i in range(length)])


def lookup_mask(mask_float, row_ids, col_ids):
    blocks = mask_float.shape[0]
    block_iota = jnp.arange(blocks, dtype=jnp.int32)
    row_hot = (row_ids[:, None] == block_iota[None, :]).astype(jnp.float32)
    col_hot = (col_ids[:, None] == block_iota[None, :]).astype(jnp.float32)
    picked = jnp.dot(row_hot, mask_float, precision=lax.Precision.HIGHEST)
    return jnp.sum(picked * col_hot, axis=1) > 0.5


def choose(flag, moved, held):
    return jax.tree.map(lambda first, second: jnp.where(flag, first, second), moved, held)


def contribution(
    left_pair, left_region, right_pair, right_region, own_labels, block_rows, block_cols
):
    left_tiles, left_labels = left_pair
    right_tiles, right_labels = right_pair
    slot_count = left_tiles.shape[0]
    side = left_tiles.shape[1]
    left_ids = left_labels.astype(jnp.int32)
    right_ids = right_labels.astype(jnp.int32)
    own_ids = own_labels.astype(jnp.int32)
    left_live = left_ids >= 0
    right_live = right_ids >= 0
    own_live = own_ids >= 0
    left_row = left_ids // block_cols
    left_inner = left_region * block_cols + left_ids % block_cols
    right_inner = right_region * block_rows + right_ids // block_cols
    right_col = right_ids % block_cols
    own_row = own_ids // block_cols
    own_col = own_ids % block_cols
    matched = own_live[:, None, None] & left_live[None, :, None] & right_live[None, None, :]
    matched = matched & (left_row[None, :, None] == own_row[:, None, None])
    matched = matched & (left_inner[None, :, None] == right_inner[None, None, :])
    matched = matched & (right_col[None, None, :] == own_col[:, None, None])
    matched_int = matched.astype(jnp.int32)
    right_places = jnp.arange(slot_count, dtype=jnp.int32)
    index = jnp.sum(matched_int * right_places[None, None, :], axis=2, dtype=jnp.int32)
    present = jnp.sum(matched_int, axis=2, dtype=jnp.int32)
    picked = jnp.take(right_tiles, index.reshape(slot_count * slot_count), axis=0)
    picked = (
        picked.reshape(slot_count, slot_count, side, side)
        * present.astype(jnp.bfloat16)[:, :, None, None]
    )
    return jnp.einsum("ixy,siyz->sxz", left_tiles, picked, preferred_element_type=jnp.float32)


def local(tiles, stack_index, block_mask):
    row_size = lax.axis_size("row")
    col_size = lax.axis_size("col")
    band_row = lax.axis_index("row")
    band_col = lax.axis_index("col")
    block_rows = NB // row_size
    block_cols = NB // col_size
    steps = max(row_size, col_size)
    left_group = steps // col_size
    right_group = steps // row_size
    mask_float = block_mask.astype(jnp.float32)
    own_ids = stack_index[0, 0]
    own_stack = tiles[0, 0]
    own_valid = lookup_mask(
        mask_float,
        band_row * block_rows + own_ids // block_cols,
        band_col * block_cols + own_ids % block_cols,
    )
    own_labels = jnp.where(own_valid, own_ids, -1).astype(jnp.bfloat16)
    left_offset = right_group * band_row // left_group % col_size
    right_offset = left_group * band_col // right_group % row_size
    left_start = (band_col + left_offset) % col_size
    right_start = (band_row + right_offset) % row_size
    panel_start = (left_group * band_col + right_group * band_row) % steps

    def skew_left(pair):
        for bit in range((col_size - 1).bit_length()):
            moved = jax.tree.map(
                lambda part, own: part.astype(own.dtype),
                shifted(shortened(pair), "col", -(1 << bit)),
                pair,
            )
            pair = choose(left_offset // (1 << bit) % 2 == 1, moved, pair)
        return pair

    def advance(carry_state, left_moved, right_moved, heading):
        left_pair, right_pair, left_region, right_region, panel = carry_state
        if heading > 0:
            take_left = (panel + 1) % left_group == 0
            take_right = (panel + 1) % right_group == 0
        else:
            take_left = panel % left_group == 0
            take_right = panel % right_group == 0
        left_pair = choose(take_left, left_moved, left_pair)
        right_pair = choose(take_right, right_moved, right_pair)
        left_region = jnp.where(take_left, (left_region + heading) % col_size, left_region)
        right_region = jnp.where(take_right, (right_region + heading) % row_size, right_region)
        panel = (panel + heading) % steps
        return (left_pair, right_pair, left_region, right_region, panel)

    def local_term(carry_state):
        return contribution(
            carry_state[0],
            carry_state[2],
            carry_state[1],
            carry_state[3],
            own_labels,
            block_rows,
            block_cols,
        )

    def multiply(left_pair, right_pair):
        start_state = (left_pair, right_pair, left_start, right_start, panel_start)
        total = local_term(start_state)

        def forward_turn(carry_state):
            left_moved = shifted(shortened(carry_state[0]), "col", -1)
            right_moved = shifted(shortened(carry_state[1]), "row", -1)
            return advance(carry_state, left_moved, right_moved, 1)

        def backward_turn(carry_state):
            left_moved = shifted(shortened(carry_state[0]), "col", 1)
            right_moved = shifted(shortened(carry_state[1]), "row", 1)
            return advance(carry_state, left_moved, right_moved, -1)

        backward_count = (steps - 1) // 2

        def paired_turn(turn_index, carry):
            running, ahead_state, behind_state = carry
            ahead_state = forward_turn(ahead_state)
            behind_state = backward_turn(behind_state)
            running = running + local_term(ahead_state) + local_term(behind_state)
            return (running, ahead_state, behind_state)

        total, ahead_state, behind_state = lax.fori_loop(
            0, backward_count, paired_turn, (total, start_state, start_state)
        )
        ahead_state = forward_turn(ahead_state)
        total = total + local_term(ahead_state)
        return total

    own_pair = (own_stack, own_labels)
    pair = own_pair
    for bit in range((row_size - 1).bit_length()):
        moved = jax.tree.map(
            lambda part, own: part.astype(own.dtype),
            shifted(shortened(pair), "row", -(1 << bit)),
            pair,
        )
        pair = choose(right_offset // (1 << bit) % 2 == 1, moved, pair)
    square = multiply(skew_left(own_pair), pair).astype(jnp.bfloat16)
    pair = own_pair
    for bit in range((row_size - 1).bit_length()):
        moved = jax.tree.map(
            lambda part, own: part.astype(own.dtype),
            shifted(shortened(pair), "row", -(1 << bit)),
            pair,
        )
        pair = choose(right_offset // (1 << bit) % 2 == 1, moved, pair)
    cube_sum = multiply(skew_left((square, own_labels)), pair)
    valid_float = own_valid.astype(jnp.float32)
    purified = (3.0 * square.astype(jnp.float32) - 2.0 * cube_sum) * valid_float[:, None, None]
    return purified.astype(jnp.bfloat16)[None, None]


def solution(mesh):
    placed = (P("row", "col", None, None, None), P("row", "col", None), P())
    return jax.shard_map(
        local,
        mesh=mesh,
        in_specs=placed,
        out_specs=P("row", "col", None, None, None),
        check_vma=False,
    )
```

profile of v0, /device:TPU:1, one launch (start us, length us, event | category | flops | bytes accessed | tf_op | source)
XLA Modules:
  0.0 330.0 jit_solution(5636628191618418072)
XLA Ops:
  1.2 5.7 %collective-permute-start.16 = (bf16[3,256,256]{1,2,0:T(8,128)(2,1)S(1)}, bf16[3,256,256]{1,2,0:T(8,128)(2,1)S(1)}, u32[]{:S(2)}, u32[]{:S(2)}) collective-permute-start(bf16[3,256,256]{1,2,0:T(8,128)(2,1)S(1)} %bitcast.134), channel_id=1, source_target_pairs={{0,28},{4,0},{8,4},{12,8},{16,12},{20,16},{24,20},{28,24},{1,29},{... | collective-permute-start | bytes 1179656 | tf_op jit(solution)/shard_map/ppermute | solution.py:19
  16.4 2.1 collective-permute-start.20
  20.3 3.1 collective-permute-done.23
  24.5 2.1 collective-permute-start.25
  26.7 3.6 %collective-permute-done.17 = bf16[3,256,256]{1,2,0:T(8,128)(2,1)S(1)} collective-permute-done((bf16[3,256,256]{1,2,0:T(8,128)(2,1)S(1)}, bf16[3,256,256]{1,2,0:T(8,128)(2,1)S(1)}, u32[]{:S(2)}, u32[]{:S(2)}) %collective-permute-start.17) | collective-permute-done | bytes 393248 | tf_op jit(solution)/shard_map/ppermute | solution.py:19
  33.1 16.6 %collective-permute-done.18 = bf16[3,256,256]{1,2,0:T(8,128)(2,1)S(1)} collective-permute-done((bf16[3,256,256]{1,2,0:T(8,128)(2,1)S(1)}, bf16[3,256,256]{1,2,0:T(8,128)(2,1)S(1)}, u32[]{:S(2)}, u32[]{:S(2)}) %collective-permute-start.18) | collective-permute-done | bytes 393248 | tf_op jit(solution)/shard_map/ppermute | solution.py:19
  50.6 1.8 copy.64
  52.4 1.8 copy.71
  55.0 1.4 convolution_bitcast_fusion.7
  56.4 104.9 %while.82 = (s32[]{:T(128)}, f32[3,256,256]{1,2,0:T(8,128)}, bf16[3,256,256]{2,1,0:T(8,128)(2,1)S(1)}, bf16[3]{0:T(256)(128)(2,1)S(1)}, bf16[3,256,256]{2,1,0:T(...) while((s32[]{:T(128)}, f32[3,256,256]{1,2,0:T(8,128)}, ...), condition=%wide.region_8.10_spmd, body=%wide.region_3.9_spmd.sunk | while | flops 607128576 | bytes 41692284 | solution.py:154
  56.4 3.1 collective-permute-start
  59.5 5.1 %collective-permute-start.1 = (bf16[3]{0:T(256)(128)(2,1)}, bf16[3]{0:T(256)(128)(2,1)S(1)}, u32[]{:S(2)}, u32[]{:S(2)}) collective-permute-start(bf16[3]{0:T(256)(128)(2,1)} %get-tuple-element.1164), channel_id=1, source_target_pairs={{0,28},{4,0},{8,4},{12,8},{16,12},{20,16},{24,20},{28,24},{1,29},{... | collective-permute-start | bytes 26 | tf_op jit(solution)/shard_map/while/body/eval_jaxpr/ppermute | solution.py:19
  65.4 1.6 collective-permute-start.4
  68.8 4.5 %collective-permute-start.6 = (bf16[3,256,256]{2,1,0:T(8,128)(2,1)}, bf16[3,256,256]{2,1,0:T(8,128)(2,1)S(1)}, u32[]{:S(2)}, u32[]{:S(2)}) collective-permute-start(bf16[3,256,256]{2,1,0:T(8,128)(2,1)} %get-tuple-element.1163), channel_id=1, source_target_pairs={{0,28},{4,0},{8,4},{12,8},{16,12},{20,16},{24,20},{28,24},{1,29},{... | collective-permute-start | bytes 1179656 | tf_op jit(solution)/shard_map/while/body/eval_jaxpr/ppermute | solution.py:19
  80.9 1.6 copy.56
  85.0 1.9 broadcast_select_fusion.44
  86.9 1.5 convolution_bitcast_fusion.10
  91.9 4.2 %collective-permute-start.1 = (bf16[3]{0:T(256)(128)(2,1)}, bf16[3]{0:T(256)(128)(2,1)S(1)}, u32[]{:S(2)}, u32[]{:S(2)}) collective-permute-start(bf16[3]{0:T(256)(128)(2,1)} %get-tuple-element.1164), channel_id=1, source_target_pairs={{0,28},{4,0},{8,4},{12,8},{16,12},{20,16},{24,20},{28,24},{1,29},{... | collective-permute-start | bytes 26 | tf_op jit(solution)/shard_map/while/body/eval_jaxpr/ppermute | solution.py:19
  98.3 2.0 collective-permute-start.4
  102.1 4.5 %collective-permute-start.6 = (bf16[3,256,256]{2,1,0:T(8,128)(2,1)}, bf16[3,256,256]{2,1,0:T(8,128)(2,1)S(1)}, u32[]{:S(2)}, u32[]{:S(2)}) collective-permute-start(bf16[3,256,256]{2,1,0:T(8,128)(2,1)} %get-tuple-element.1163), channel_id=1, source_target_pairs={{0,28},{4,0},{8,4},{12,8},{16,12},{20,16},{24,20},{28,24},{1,29},{... | collective-permute-start | bytes 1179656 | tf_op jit(solution)/shard_map/while/body/eval_jaxpr/ppermute | solution.py:19
  115.1 1.6 copy.56
  118.8 1.9 broadcast_select_fusion.44
  120.7 1.5 convolution_bitcast_fusion.10
  126.1 3.9 %collective-permute-start.1 = (bf16[3]{0:T(256)(128)(2,1)}, bf16[3]{0:T(256)(128)(2,1)S(1)}, u32[]{:S(2)}, u32[]{:S(2)}) collective-permute-start(bf16[3]{0:T(256)(128)(2,1)} %get-tuple-element.1164), channel_id=1, source_target_pairs={{0,28},{4,0},{8,4},{12,8},{16,12},{20,16},{24,20},{28,24},{1,29},{... | collective-permute-start | bytes 26 | tf_op jit(solution)/shard_map/while/body/eval_jaxpr/ppermute | solution.py:19
  129.9 3.5 %collective-permute-start.2 = (bf16[3]{0:T(256)(128)(2,1)}, bf16[3]{0:T(256)(128)(2,1)S(1)}, u32[]{:S(2)}, u32[]{:S(2)}) collective-permute-start(bf16[3]{0:T(256)(128)(2,1)} %get-tuple-element.1171), channel_id=1, source_target_pairs={{0,4},{4,8},{8,12},{12,16},{16,20},{20,24},{24,28},{28,0},{1,5},{5... | collective-permute-start | bytes 26 | tf_op jit(solution)/shard_map/while/body/eval_jaxpr/ppermute | solution.py:19
  133.5 2.5 collective-permute-start.3
  138.4 4.5 %collective-permute-start.6 = (bf16[3,256,256]{2,1,0:T(8,128)(2,1)}, bf16[3,256,256]{2,1,0:T(8,128)(2,1)S(1)}, u32[]{:S(2)}, u32[]{:S(2)}) collective-permute-start(bf16[3,256,256]{2,1,0:T(8,128)(2,1)} %get-tuple-element.1163), channel_id=1, source_target_pairs={{0,28},{4,0},{8,4},{12,8},{16,12},{20,16},{24,20},{28,24},{1,29},{... | collective-permute-start | bytes 1179656 | tf_op jit(solution)/shard_map/while/body/eval_jaxpr/ppermute | solution.py:19
  144.2 1.4 collective-permute-start.7
  150.7 1.6 copy.56
  154.5 1.9 broadcast_select_fusion.44
  156.4 1.5 convolution_bitcast_fusion.10
  161.3 3.2 collective-permute-start.26
  164.6 2.2 collective-permute-start.27
  166.7 1.7 collective-permute-start.29
  168.4 4.1 %collective-permute-done.28 = bf16[3]{0:T(256)(128)(2,1)S(1)} collective-permute-done((bf16[3]{0:T(256)(128)(2,1)}, bf16[3]{0:T(256)(128)(2,1)S(1)}, u32[]{:S(2)}, u32[]{:S(2)}) %collective-permute-start.28) | collective-permute-done | bytes 38 | tf_op jit(solution)/shard_map/ppermute | solution.py:19
  178.0 1.9 collective-permute-start.30
  179.9 11.7 %collective-permute-done.30 = bf16[3,256,256]{1,2,0:T(8,128)(2,1)S(1)} collective-permute-done((bf16[3,256,256]{1,2,0:T(8,128)(2,1)S(1)}, bf16[3,256,256]{1,2,0:T(8,128)(2,1)S(1)}, u32[]{:S(2)}, u32[]{:S(2)}) %collective-permute-start.30) | collective-permute-done | bytes 393248 | tf_op jit(solution)/shard_map/ppermute | solution.py:19
  194.0 8.8 %collective-permute-done.31 = bf16[3,256,256]{1,2,0:T(8,128)(2,1)S(1)} collective-permute-done((bf16[3,256,256]{1,2,0:T(8,128)(2,1)S(1)}, bf16[3,256,256]{1,2,0:T(8,128)(2,1)S(1)}, u32[]{:S(2)}, u32[]{:S(2)}) %collective-permute-start.31) | collective-permute-done | bytes 393248 | tf_op jit(solution)/shard_map/ppermute | solution.py:19
  202.8 1.4 convolution_bitcast_fusion.5
  205.2 106.2 %while.83 = (s32[]{:T(128)}, f32[3,256,256]{1,2,0:T(8,128)}, bf16[3,256,256]{2,1,0:T(8,128)(2,1)S(1)}, bf16[3]{0:T(256)(128)(2,1)S(1)}, bf16[3,256,256]{2,1,0:T(...) while((s32[]{:T(128)}, f32[3,256,256]{1,2,0:T(8,128)}, ...), condition=%wide.region_16.18_spmd, body=%wide.region_11.17_spmd.sunk | while | flops 607128576 | bytes 41692396 | solution.py:154
  205.2 2.2 collective-permute-start.8
  207.4 1.9 collective-permute-start.9
  212.7 4.2 %collective-permute-start.14 = (bf16[3,256,256]{2,1,0:T(8,128)(2,1)}, bf16[3,256,256]{2,1,0:T(8,128)(2,1)S(1)}, u32[]{:S(2)}, u32[]{:S(2)}) collective-permute-start(bf16[3,256,256]{2,1,0:T(8,128)(2,1)} %get-tuple-element.1241), channel_id=1, source_target_pairs={{0,28},{4,0},{8,4},{12,8},{16,12},{20,16},{24,20},{28,24},{1,29},{... | collective-permute-start | bytes 1179656 | tf_op jit(solution)/shard_map/while/body/eval_jaxpr/ppermute | solution.py:19
  218.1 7.2 %collective-permute-start.15 = (bf16[3,256,256]{2,1,0:T(8,128)(2,1)S(1)}, bf16[3,256,256]{2,1,0:T(8,128)(2,1)}, u32[]{:S(2)}, u32[]{:S(2)}) collective-permute-start(bf16[3,256,256]{2,1,0:T(8,128)(2,1)S(1)} %get-tuple-element.1239), channel_id=1, source_target_pairs={{0,3},{1,0},{2,1},{3,2},{4,7},{5,4},{6,5},{7,6},{8,11},{9,8},{10,9... | collective-permute-start | bytes 1179656 | tf_op jit(solution)/shard_map/while/body/eval_jaxpr/ppermute | solution.py:19
  230.5 1.5 copy.58
  234.2 1.9 broadcast_select_fusion.48
  236.1 1.5 convolution_bitcast_fusion.11
  240.5 2.3 collective-permute-start.8
  242.9 1.8 collective-permute-start.9
  248.0 4.0 %collective-permute-start.14 = (bf16[3,256,256]{2,1,0:T(8,128)(2,1)}, bf16[3,256,256]{2,1,0:T(8,128)(2,1)S(1)}, u32[]{:S(2)}, u32[]{:S(2)}) collective-permute-start(bf16[3,256,256]{2,1,0:T(8,128)(2,1)} %get-tuple-element.1241), channel_id=1, source_target_pairs={{0,28},{4,0},{8,4},{12,8},{16,12},{20,16},{24,20},{28,24},{1,29},{... | collective-permute-start | bytes 1179656 | tf_op jit(solution)/shard_map/while/body/eval_jaxpr/ppermute | solution.py:19
  252.0 1.9 collective-permute-done.10
  253.9 6.8 %collective-permute-start.15 = (bf16[3,256,256]{2,1,0:T(8,128)(2,1)S(1)}, bf16[3,256,256]{2,1,0:T(8,128)(2,1)}, u32[]{:S(2)}, u32[]{:S(2)}) collective-permute-start(bf16[3,256,256]{2,1,0:T(8,128)(2,1)S(1)} %get-tuple-element.1239), channel_id=1, source_target_pairs={{0,3},{1,0},{2,1},{3,2},{4,7},{5,4},{6,5},{7,6},{8,11},{9,8},{10,9... | collective-permute-start | bytes 1179656 | tf_op jit(solution)/shard_map/while/body/eval_jaxpr/ppermute | solution.py:19
  265.9 1.5 copy.58
  269.7 1.9 broadcast_select_fusion.48
  271.6 1.5 convolution_bitcast_fusion.11
  276.1 2.1 collective-permute-start.8
  278.2 2.0 collective-permute-start.9
  283.6 4.0 %collective-permute-start.14 = (bf16[3,256,256]{2,1,0:T(8,128)(2,1)}, bf16[3,256,256]{2,1,0:T(8,128)(2,1)S(1)}, u32[]{:S(2)}, u32[]{:S(2)}) collective-permute-start(bf16[3,256,256]{2,1,0:T(8,128)(2,1)} %get-tuple-element.1241), channel_id=1, source_target_pairs={{0,28},{4,0},{8,4},{12,8},{16,12},{20,16},{24,20},{28,24},{1,29},{... | collective-permute-start | bytes 1179656 | tf_op jit(solution)/shard_map/while/body/eval_jaxpr/ppermute | solution.py:19
  287.6 1.9 collective-permute-done.10
  289.5 6.6 %collective-permute-start.15 = (bf16[3,256,256]{2,1,0:T(8,128)(2,1)S(1)}, bf16[3,256,256]{2,1,0:T(8,128)(2,1)}, u32[]{:S(2)}, u32[]{:S(2)}) collective-permute-start(bf16[3,256,256]{2,1,0:T(8,128)(2,1)S(1)} %get-tuple-element.1239), channel_id=1, source_target_pairs={{0,3},{1,0},{2,1},{3,2},{4,7},{5,4},{6,5},{7,6},{8,11},{9,8},{10,9... | collective-permute-start | bytes 1179656 | tf_op jit(solution)/shard_map/while/body/eval_jaxpr/ppermute | solution.py:19
  301.3 1.5 copy.58
  305.0 1.9 broadcast_select_fusion.48
  306.9 1.5 convolution_bitcast_fusion.11
  311.6 11.8 %collective-permute-done.34 = bf16[3]{0:T(256)(128)(2,1)S(1)} collective-permute-done((bf16[3]{0:T(256)(128)(2,1)S(1)}, bf16[3]{0:T(256)(128)(2,1)S(1)}, u32[]{:S(2)}, u32[]{:S(2)}) %collective-permute-start.34) | collective-permute-done | bytes 38 | tf_op jit(solution)/shard_map/ppermute | solution.py:19
  (479 shorter events, 123.8 us)
Async XLA Ops:
  1.2 22.4 %collective-permute-start.24 = (bf16[3,256,256]{1,2,0:T(8,128)(2,1)S(1)}, bf16[3,256,256]{1,2,0:T(8,128)(2,1)S(1)}, u32[]{:S(2)}, u32[]{:S(2)}) collective-permute-start(bf16[3,256,256]{1,2,0:T(8,128)(2,1)S(1)} %bitcast.133), channel_id=1, source_target_pairs={{0,3},{1,0},{2,1},{3,2},{4,7},{5,4},{6,5},{7,6},{8,11},{9,8},{10,9... | collective-permute-start | bytes 1179656 | tf_op jit(solution)/shard_map/ppermute | solution.py:19
  1.2 22.3 %collective-permute-start.16 = (bf16[3,256,256]{1,2,0:T(8,128)(2,1)S(1)}, bf16[3,256,256]{1,2,0:T(8,128)(2,1)S(1)}, u32[]{:S(2)}, u32[]{:S(2)}) collective-permute-start(bf16[3,256,256]{1,2,0:T(8,128)(2,1)S(1)} %bitcast.134), channel_id=1, source_target_pairs={{0,28},{4,0},{8,4},{12,8},{16,12},{20,16},{24,20},{28,24},{1,29},{... | collective-permute-start | bytes 1179656 | tf_op jit(solution)/shard_map/ppermute | solution.py:19
  9.9 3.5 %collective-permute-start.19 = (bf16[3]{0:T(256)(128)(2,1)}, bf16[3]{0:T(256)(128)(2,1)S(1)}, u32[]{:S(2)}, u32[]{:S(2)}) collective-permute-start(bf16[3]{0:T(256)(128)(2,1)} %get-tuple-element.1227), channel_id=1, source_target_pairs={{0,3},{1,0},{2,1},{3,2},{4,7},{5,4},{6,5},{7,6},{8,11},{9,8},{10,9... | collective-permute-start | bytes 26 | tf_op jit(solution)/shard_map/ppermute | solution.py:19
  11.2 3.3 %collective-permute-start.21 = (bf16[3]{0:T(256)(128)(2,1)}, bf16[3]{0:T(256)(128)(2,1)S(1)}, u32[]{:S(2)}, u32[]{:S(2)}) collective-permute-start(bf16[3]{0:T(256)(128)(2,1)} %get-tuple-element.1227), channel_id=1, source_target_pairs={{0,28},{4,0},{8,4},{12,8},{16,12},{20,16},{24,20},{28,24},{1,29},{... | collective-permute-start | bytes 26 | tf_op jit(solution)/shard_map/ppermute | solution.py:19
  15.1 4.9 %collective-permute-start.22 = (bf16[3]{0:T(256)(128)(2,1)S(1)}, bf16[3]{0:T(256)(128)(2,1)S(1)}, u32[]{:S(2)}, u32[]{:S(2)}) collective-permute-start(bf16[3]{0:T(256)(128)(2,1)S(1)} %get-tuple-element.820), channel_id=1, source_target_pairs={{0,24},{4,28},{8,0},{12,4},{16,8},{20,12},{24,16},{28,20},{1,25},{... | collective-permute-start | bytes 26 | tf_op jit(solution)/shard_map/ppermute | solution.py:19
  16.4 3.1 collective-permute-start.20
  20.1 3.4 %collective-permute-start.23 = (bf16[3]{0:T(256)(128)(2,1)S(1)}, bf16[3]{0:T(256)(128)(2,1)S(1)}, u32[]{:S(2)}, u32[]{:S(2)}) collective-permute-start(bf16[3]{0:T(256)(128)(2,1)S(1)} %broadcast_select_fusion.25), channel_id=1, source_target_pairs={{0,16},{4,20},{8,24},{12,28},{16,0},{20,4},{24,8},{28,12},{1,17},{... | collective-permute-start | bytes 26 | tf_op jit(solution)/shard_map/ppermute | solution.py:19
  23.6 6.7 %collective-permute-start.17 = (bf16[3,256,256]{1,2,0:T(8,128)(2,1)S(1)}, bf16[3,256,256]{1,2,0:T(8,128)(2,1)S(1)}, u32[]{:S(2)}, u32[]{:S(2)}) collective-permute-start(bf16[3,256,256]{1,2,0:T(8,128)(2,1)S(1)} %get-tuple-element.805), channel_id=1, source_target_pairs={{0,24},{4,28},{8,0},{12,4},{16,8},{20,12},{24,16},{28,20},{1,25},{... | collective-permute-start | bytes 1179656 | tf_op jit(solution)/shard_map/ppermute | solution.py:19
  24.5 7.6 %collective-permute-start.25 = (bf16[3,256,256]{1,2,0:T(8,128)(2,1)S(1)}, bf16[3,256,256]{1,2,0:T(8,128)(2,1)S(1)}, u32[]{:S(2)}, u32[]{:S(2)}) collective-permute-start(bf16[3,256,256]{1,2,0:T(8,128)(2,1)S(1)} %get-tuple-element.804), channel_id=1, source_target_pairs={{0,2},{1,3},{2,0},{3,1},{4,6},{5,7},{6,4},{7,5},{8,10},{9,11},{10,... | collective-permute-start | bytes 1179656 | tf_op jit(solution)/shard_map/ppermute | solution.py:19
  30.4 19.3 %collective-permute-start.18 = (bf16[3,256,256]{1,2,0:T(8,128)(2,1)S(1)}, bf16[3,256,256]{1,2,0:T(8,128)(2,1)S(1)}, u32[]{:S(2)}, u32[]{:S(2)}) collective-permute-start(bf16[3,256,256]{1,2,0:T(8,128)(2,1)S(1)} %broadcast_select_fusion.20), channel_id=1, source_target_pairs={{0,16},{4,20},{8,24},{12,28},{16,0},{20,4},{24,8},{28,12},{1,17},{... | collective-permute-start | bytes 1179656 | tf_op jit(solution)/shard_map/ppermute | solution.py:19
  56.4 23.0 %collective-permute-start = (bf16[3,256,256]{2,1,0:T(8,128)(2,1)}, bf16[3,256,256]{2,1,0:T(8,128)(2,1)S(1)}, u32[]{:S(2)}, u32[]{:S(2)}) collective-permute-start(bf16[3,256,256]{2,1,0:T(8,128)(2,1)} %get-tuple-element.1170), channel_id=1, source_target_pairs={{0,4},{4,8},{8,12},{12,16},{16,20},{20,24},{24,28},{28,0},{1,5},{5... | collective-permute-start | bytes 1179656 | tf_op jit(solution)/shard_map/while/body/eval_jaxpr/ppermute | solution.py:19
  59.5 16.3 %collective-permute-start.1 = (bf16[3]{0:T(256)(128)(2,1)}, bf16[3]{0:T(256)(128)(2,1)S(1)}, u32[]{:S(2)}, u32[]{:S(2)}) collective-permute-start(bf16[3]{0:T(256)(128)(2,1)} %get-tuple-element.1164), channel_id=1, source_target_pairs={{0,28},{4,0},{8,4},{12,8},{16,12},{20,16},{24,20},{28,24},{1,29},{... | collective-permute-start | bytes 26 | tf_op jit(solution)/shard_map/while/body/eval_jaxpr/ppermute | solution.py:19
  64.6 9.9 %collective-permute-start.2 = (bf16[3]{0:T(256)(128)(2,1)}, bf16[3]{0:T(256)(128)(2,1)S(1)}, u32[]{:S(2)}, u32[]{:S(2)}) collective-permute-start(bf16[3]{0:T(256)(128)(2,1)} %get-tuple-element.1171), channel_id=1, source_target_pairs={{0,4},{4,8},{8,12},{12,16},{16,20},{20,24},{24,28},{28,0},{1,5},{5... | collective-permute-start | bytes 26 | tf_op jit(solution)/shard_map/while/body/eval_jaxpr/ppermute | solution.py:19
  64.6 3.9 %collective-permute-start.3 = (bf16[3]{0:T(256)(128)(2,1)S(1)}, bf16[3]{0:T(256)(128)(2,1)S(1)}, u32[]{:S(2)}, u32[]{:S(2)}) collective-permute-start(bf16[3]{0:T(256)(128)(2,1)S(1)} %get-tuple-element.1162), channel_id=1, source_target_pairs={{0,3},{1,0},{2,1},{3,2},{4,7},{5,4},{6,5},{7,6},{8,11},{9,8},{10,9... | collective-permute-start | bytes 26 | tf_op jit(solution)/shard_map/while/body/eval_jaxpr/ppermute | solution.py:19
  65.4 3.4 %collective-permute-start.4 = (bf16[3]{0:T(256)(128)(2,1)}, bf16[3]{0:T(256)(128)(2,1)S(1)}, u32[]{:S(2)}, u32[]{:S(2)}) collective-permute-start(bf16[3]{0:T(256)(128)(2,1)} %get-tuple-element.1169), channel_id=1, source_target_pairs={{0,1},{1,2},{2,3},{3,0},{4,5},{5,6},{6,7},{7,4},{8,9},{9,10},{10,1... | collective-permute-start | bytes 26 | tf_op jit(solution)/shard_map/while/body/eval_jaxpr/ppermute | solution.py:19
  68.5 16.5 %collective-permute-start.5 = (bf16[3,256,256]{2,1,0:T(8,128)(2,1)}, bf16[3,256,256]{2,1,0:T(8,128)(2,1)}, u32[]{:S(2)}, u32[]{:S(2)}) collective-permute-start(bf16[3,256,256]{2,1,0:T(8,128)(2,1)} %get-tuple-element.1168), channel_id=1, source_target_pairs={{0,1},{1,2},{2,3},{3,0},{4,5},{5,6},{6,7},{7,4},{8,9},{9,10},{10,1... | collective-permute-start | bytes 1179656 | tf_op jit(solution)/shard_map/while/body/eval_jaxpr/ppermute | solution.py:19
  68.8 14.1 %collective-permute-start.6 = (bf16[3,256,256]{2,1,0:T(8,128)(2,1)}, bf16[3,256,256]{2,1,0:T(8,128)(2,1)S(1)}, u32[]{:S(2)}, u32[]{:S(2)}) collective-permute-start(bf16[3,256,256]{2,1,0:T(8,128)(2,1)} %get-tuple-element.1163), channel_id=1, source_target_pairs={{0,28},{4,0},{8,4},{12,8},{16,12},{20,16},{24,20},{28,24},{1,29},{... | collective-permute-start | bytes 1179656 | tf_op jit(solution)/shard_map/while/body/eval_jaxpr/ppermute | solution.py:19
  74.5 13.9 %collective-permute-start.7 = (bf16[3,256,256]{2,1,0:T(8,128)(2,1)S(1)}, bf16[3,256,256]{2,1,0:T(8,128)(2,1)}, u32[]{:S(2)}, u32[]{:S(2)}) collective-permute-start(bf16[3,256,256]{2,1,0:T(8,128)(2,1)S(1)} %get-tuple-element.1161), channel_id=1, source_target_pairs={{0,3},{1,0},{2,1},{3,2},{4,7},{5,4},{6,5},{7,6},{8,11},{9,8},{10,9... | collective-permute-start | bytes 1179656 | tf_op jit(solution)/shard_map/while/body/eval_jaxpr/ppermute | solution.py:19
  91.9 21.8 %collective-permute-start = (bf16[3,256,256]{2,1,0:T(8,128)(2,1)}, bf16[3,256,256]{2,1,0:T(8,128)(2,1)S(1)}, u32[]{:S(2)}, u32[]{:S(2)}) collective-permute-start(bf16[3,256,256]{2,1,0:T(8,128)(2,1)} %get-tuple-element.1170), channel_id=1, source_target_pairs={{0,4},{4,8},{8,12},{12,16},{16,20},{20,24},{24,28},{28,0},{1,5},{5... | collective-permute-start | bytes 1179656 | tf_op jit(solution)/shard_map/while/body/eval_jaxpr/ppermute | solution.py:19
  91.9 18.1 %collective-permute-start.1 = (bf16[3]{0:T(256)(128)(2,1)}, bf16[3]{0:T(256)(128)(2,1)S(1)}, u32[]{:S(2)}, u32[]{:S(2)}) collective-permute-start(bf16[3]{0:T(256)(128)(2,1)} %get-tuple-element.1164), channel_id=1, source_target_pairs={{0,28},{4,0},{8,4},{12,8},{16,12},{20,16},{24,20},{28,24},{1,29},{... | collective-permute-start | bytes 26 | tf_op jit(solution)/shard_map/while/body/eval_jaxpr/ppermute | solution.py:19
  96.0 12.5 %collective-permute-start.2 = (bf16[3]{0:T(256)(128)(2,1)}, bf16[3]{0:T(256)(128)(2,1)S(1)}, u32[]{:S(2)}, u32[]{:S(2)}) collective-permute-start(bf16[3]{0:T(256)(128)(2,1)} %get-tuple-element.1171), channel_id=1, source_target_pairs={{0,4},{4,8},{8,12},{12,16},{16,20},{20,24},{24,28},{28,0},{1,5},{5... | collective-permute-start | bytes 26 | tf_op jit(solution)/shard_map/while/body/eval_jaxpr/ppermute | solution.py:19
  97.2 4.6 %collective-permute-start.3 = (bf16[3]{0:T(256)(128)(2,1)S(1)}, bf16[3]{0:T(256)(128)(2,1)S(1)}, u32[]{:S(2)}, u32[]{:S(2)}) collective-permute-start(bf16[3]{0:T(256)(128)(2,1)S(1)} %get-tuple-element.1162), channel_id=1, source_target_pairs={{0,3},{1,0},{2,1},{3,2},{4,7},{5,4},{6,5},{7,6},{8,11},{9,8},{10,9... | collective-permute-start | bytes 26 | tf_op jit(solution)/shard_map/while/body/eval_jaxpr/ppermute | solution.py:19
  98.3 3.8 %collective-permute-start.4 = (bf16[3]{0:T(256)(128)(2,1)}, bf16[3]{0:T(256)(128)(2,1)S(1)}, u32[]{:S(2)}, u32[]{:S(2)}) collective-permute-start(bf16[3]{0:T(256)(128)(2,1)} %get-tuple-element.1169), channel_id=1, source_target_pairs={{0,1},{1,2},{2,3},{3,0},{4,5},{5,6},{6,7},{7,4},{8,9},{9,10},{10,1... | collective-permute-start | bytes 26 | tf_op jit(solution)/shard_map/while/body/eval_jaxpr/ppermute | solution.py:19
  101.8 17.0 %collective-permute-start.5 = (bf16[3,256,256]{2,1,0:T(8,128)(2,1)}, bf16[3,256,256]{2,1,0:T(8,128)(2,1)}, u32[]{:S(2)}, u32[]{:S(2)}) collective-permute-start(bf16[3,256,256]{2,1,0:T(8,128)(2,1)} %get-tuple-element.1168), channel_id=1, source_target_pairs={{0,1},{1,2},{2,3},{3,0},{4,5},{5,6},{6,7},{7,4},{8,9},{9,10},{10,1... | collective-permute-start | bytes 1179656 | tf_op jit(solution)/shard_map/while/body/eval_jaxpr/ppermute | solution.py:19
  102.1 14.6 %collective-permute-start.6 = (bf16[3,256,256]{2,1,0:T(8,128)(2,1)}, bf16[3,256,256]{2,1,0:T(8,128)(2,1)S(1)}, u32[]{:S(2)}, u32[]{:S(2)}) collective-permute-start(bf16[3,256,256]{2,1,0:T(8,128)(2,1)} %get-tuple-element.1163), channel_id=1, source_target_pairs={{0,28},{4,0},{8,4},{12,8},{16,12},{20,16},{24,20},{28,24},{1,29},{... | collective-permute-start | bytes 1179656 | tf_op jit(solution)/shard_map/while/body/eval_jaxpr/ppermute | solution.py:19
  108.5 13.8 %collective-permute-start.7 = (bf16[3,256,256]{2,1,0:T(8,128)(2,1)S(1)}, bf16[3,256,256]{2,1,0:T(8,128)(2,1)}, u32[]{:S(2)}, u32[]{:S(2)}) collective-permute-start(bf16[3,256,256]{2,1,0:T(8,128)(2,1)S(1)} %get-tuple-element.1161), channel_id=1, source_target_pairs={{0,3},{1,0},{2,1},{3,2},{4,7},{5,4},{6,5},{7,6},{8,11},{9,8},{10,9... | collective-permute-start | bytes 1179656 | tf_op jit(solution)/shard_map/while/body/eval_jaxpr/ppermute | solution.py:19
  125.8 23.5 %collective-permute-start = (bf16[3,256,256]{2,1,0:T(8,128)(2,1)}, bf16[3,256,256]{2,1,0:T(8,128)(2,1)S(1)}, u32[]{:S(2)}, u32[]{:S(2)}) collective-permute-start(bf16[3,256,256]{2,1,0:T(8,128)(2,1)} %get-tuple-element.1170), channel_id=1, source_target_pairs={{0,4},{4,8},{8,12},{12,16},{16,20},{20,24},{24,28},{28,0},{1,5},{5... | collective-permute-start | bytes 1179656 | tf_op jit(solution)/shard_map/while/body/eval_jaxpr/ppermute | solution.py:19
  126.1 19.5 %collective-permute-start.1 = (bf16[3]{0:T(256)(128)(2,1)}, bf16[3]{0:T(256)(128)(2,1)S(1)}, u32[]{:S(2)}, u32[]{:S(2)}) collective-permute-start(bf16[3]{0:T(256)(128)(2,1)} %get-tuple-element.1164), channel_id=1, source_target_pairs={{0,28},{4,0},{8,4},{12,8},{16,12},{20,16},{24,20},{28,24},{1,29},{... | collective-permute-start | bytes 26 | tf_op jit(solution)/shard_map/while/body/eval_jaxpr/ppermute | solution.py:19
  129.9 14.2 %collective-permute-start.2 = (bf16[3]{0:T(256)(128)(2,1)}, bf16[3]{0:T(256)(128)(2,1)S(1)}, u32[]{:S(2)}, u32[]{:S(2)}) collective-permute-start(bf16[3]{0:T(256)(128)(2,1)} %get-tuple-element.1171), channel_id=1, source_target_pairs={{0,4},{4,8},{8,12},{12,16},{16,20},{20,24},{24,28},{28,0},{1,5},{5... | collective-permute-start | bytes 26 | tf_op jit(solution)/shard_map/while/body/eval_jaxpr/ppermute | solution.py:19
  133.5 4.7 %collective-permute-start.3 = (bf16[3]{0:T(256)(128)(2,1)S(1)}, bf16[3]{0:T(256)(128)(2,1)S(1)}, u32[]{:S(2)}, u32[]{:S(2)}) collective-permute-start(bf16[3]{0:T(256)(128)(2,1)S(1)} %get-tuple-element.1162), channel_id=1, source_target_pairs={{0,3},{1,0},{2,1},{3,2},{4,7},{5,4},{6,5},{7,6},{8,11},{9,8},{10,9... | collective-permute-start | bytes 26 | tf_op jit(solution)/shard_map/while/body/eval_jaxpr/ppermute | solution.py:19
  138.1 16.3 %collective-permute-start.5 = (bf16[3,256,256]{2,1,0:T(8,128)(2,1)}, bf16[3,256,256]{2,1,0:T(8,128)(2,1)}, u32[]{:S(2)}, u32[]{:S(2)}) collective-permute-start(bf16[3,256,256]{2,1,0:T(8,128)(2,1)} %get-tuple-element.1168), channel_id=1, source_target_pairs={{0,1},{1,2},{2,3},{3,0},{4,5},{5,6},{6,7},{7,4},{8,9},{9,10},{10,1... | collective-permute-start | bytes 1179656 | tf_op jit(solution)/shard_map/while/body/eval_jaxpr/ppermute | solution.py:19
  138.4 13.9 %collective-permute-start.6 = (bf16[3,256,256]{2,1,0:T(8,128)(2,1)}, bf16[3,256,256]{2,1,0:T(8,128)(2,1)S(1)}, u32[]{:S(2)}, u32[]{:S(2)}) collective-permute-start(bf16[3,256,256]{2,1,0:T(8,128)(2,1)} %get-tuple-element.1163), channel_id=1, source_target_pairs={{0,28},{4,0},{8,4},{12,8},{16,12},{20,16},{24,20},{28,24},{1,29},{... | collective-permute-start | bytes 1179656 | tf_op jit(solution)/shard_map/while/body/eval_jaxpr/ppermute | solution.py:19
  144.2 13.8 %collective-permute-start.7 = (bf16[3,256,256]{2,1,0:T(8,128)(2,1)S(1)}, bf16[3,256,256]{2,1,0:T(8,128)(2,1)}, u32[]{:S(2)}, u32[]{:S(2)}) collective-permute-start(bf16[3,256,256]{2,1,0:T(8,128)(2,1)S(1)} %get-tuple-element.1161), channel_id=1, source_target_pairs={{0,3},{1,0},{2,1},{3,2},{4,7},{5,4},{6,5},{7,6},{8,11},{9,8},{10,9... | collective-permute-start | bytes 1179656 | tf_op jit(solution)/shard_map/while/body/eval_jaxpr/ppermute | solution.py:19
  161.3 13.8 %collective-permute-start.26 = (bf16[3,256,256]{2,1,0:T(8,128)(2,1)}, bf16[3,256,256]{2,1,0:T(8,128)(2,1)S(1)}, u32[]{:S(2)}, u32[]{:S(2)}) collective-permute-start(bf16[3,256,256]{2,1,0:T(8,128)(2,1)} %get-tuple-element.583), channel_id=1, source_target_pairs={{0,28},{4,0},{8,4},{12,8},{16,12},{20,16},{24,20},{28,24},{1,29},{... | collective-permute-start | bytes 1179656 | tf_op jit(solution)/shard_map/ppermute | solution.py:19
  164.5 7.9 %collective-permute-start.28 = (bf16[3]{0:T(256)(128)(2,1)}, bf16[3]{0:T(256)(128)(2,1)S(1)}, u32[]{:S(2)}, u32[]{:S(2)}) collective-permute-start(bf16[3]{0:T(256)(128)(2,1)} %get-tuple-element.586), channel_id=1, source_target_pairs={{0,28},{4,0},{8,4},{12,8},{16,12},{20,16},{24,20},{28,24},{1,29},{... | collective-permute-start | bytes 26 | tf_op jit(solution)/shard_map/ppermute | solution.py:19
  164.6 8.7 %collective-permute-start.27 = (bf16[3]{0:T(256)(128)(2,1)S(1)}, bf16[3]{0:T(256)(128)(2,1)S(1)}, u32[]{:S(2)}, u32[]{:S(2)}) collective-permute-start(bf16[3]{0:T(256)(128)(2,1)S(1)} %get-tuple-element.585), channel_id=1, source_target_pairs={{0,3},{1,0},{2,1},{3,2},{4,7},{5,4},{6,5},{7,6},{8,11},{9,8},{10,9... | collective-permute-start | bytes 26 | tf_op jit(solution)/shard_map/ppermute | solution.py:19
  166.7 10.0 %collective-permute-start.29 = (bf16[3,256,256]{2,1,0:T(8,128)(2,1)S(1)}, bf16[3,256,256]{2,1,0:T(8,128)(2,1)S(1)}, u32[]{:S(2)}, u32[]{:S(2)}) collective-permute-start(bf16[3,256,256]{2,1,0:T(8,128)(2,1)S(1)} %get-tuple-element.589), channel_id=1, source_target_pairs={{0,3},{1,0},{2,1},{3,2},{4,7},{5,4},{6,5},{7,6},{8,11},{9,8},{10,9... | collective-permute-start | bytes 1179656 | tf_op jit(solution)/shard_map/ppermute | solution.py:19
  178.0 13.7 %collective-permute-start.30 = (bf16[3,256,256]{1,2,0:T(8,128)(2,1)S(1)}, bf16[3,256,256]{1,2,0:T(8,128)(2,1)S(1)}, u32[]{:S(2)}, u32[]{:S(2)}) collective-permute-start(bf16[3,256,256]{1,2,0:T(8,128)(2,1)S(1)} %add_convert_fusion), channel_id=1, source_target_pairs={{0,3},{1,0},{2,1},{3,2},{4,7},{5,4},{6,5},{7,6},{8,11},{9,8},{10,9... | collective-permute-start | bytes 1179656 | tf_op jit(solution)/shard_map/ppermute | solution.py:19
  191.7 11.1 %collective-permute-start.31 = (bf16[3,256,256]{1,2,0:T(8,128)(2,1)S(1)}, bf16[3,256,256]{1,2,0:T(8,128)(2,1)S(1)}, u32[]{:S(2)}, u32[]{:S(2)}) collective-permute-start(bf16[3,256,256]{1,2,0:T(8,128)(2,1)S(1)} %broadcast_select_fusion.15), channel_id=1, source_target_pairs={{0,2},{1,3},{2,0},{3,1},{4,6},{5,7},{6,4},{7,5},{8,10},{9,11},{10,... | collective-permute-start | bytes 1179656 | tf_op jit(solution)/shard_map/ppermute | solution.py:19
  205.2 23.8 %collective-permute-start.8 = (bf16[3,256,256]{2,1,0:T(8,128)(2,1)S(1)}, bf16[3,256,256]{2,1,0:T(8,128)(2,1)S(1)}, u32[]{:S(2)}, u32[]{:S(2)}) collective-permute-start(bf16[3,256,256]{2,1,0:T(8,128)(2,1)S(1)} %get-tuple-element.1248), channel_id=1, source_target_pairs={{0,4},{4,8},{8,12},{12,16},{16,20},{20,24},{24,28},{28,0},{1,5},{5... | collective-permute-start | bytes 1179656 | tf_op jit(solution)/shard_map/while/body/eval_jaxpr/ppermute | solution.py:19
  207.4 17.9 %collective-permute-start.9 = (bf16[3]{0:T(256)(128)(2,1)S(1)}, bf16[3]{0:T(256)(128)(2,1)S(1)}, u32[]{:S(2)}, u32[]{:S(2)}) collective-permute-start(bf16[3]{0:T(256)(128)(2,1)S(1)} %get-tuple-element.1242), channel_id=1, source_target_pairs={{0,28},{4,0},{8,4},{12,8},{16,12},{20,16},{24,20},{28,24},{1,29},{... | collective-permute-start | bytes 26 | tf_op jit(solution)/shard_map/while/body/eval_jaxpr/ppermute | solution.py:19
  209.4 8.7 %collective-permute-start.10 = (bf16[3]{0:T(256)(128)(2,1)S(1)}, bf16[3]{0:T(256)(128)(2,1)S(1)}, u32[]{:S(2)}, u32[]{:S(2)}) collective-permute-start(bf16[3]{0:T(256)(128)(2,1)S(1)} %get-tuple-element.1249), channel_id=1, source_target_pairs={{0,4},{4,8},{8,12},{12,16},{16,20},{20,24},{24,28},{28,0},{1,5},{5... | collective-permute-start | bytes 26 | tf_op jit(solution)/shard_map/while/body/eval_jaxpr/ppermute | solution.py:19
  209.4 3.3 collective-permute-start.11
  212.7 21.6 %collective-permute-start.13 = (bf16[3,256,256]{2,1,0:T(8,128)(2,1)}, bf16[3,256,256]{2,1,0:T(8,128)(2,1)}, u32[]{:S(2)}, u32[]{:S(2)}) collective-permute-start(bf16[3,256,256]{2,1,0:T(8,128)(2,1)} %get-tuple-element.1246), channel_id=1, source_target_pairs={{0,1},{1,2},{2,3},{3,0},{4,5},{5,6},{6,7},{7,4},{8,9},{9,10},{10,1... | collective-permute-start | bytes 1179656 | tf_op jit(solution)/shard_map/while/body/eval_jaxpr/ppermute | solution.py:19
  212.7 19.4 %collective-permute-start.14 = (bf16[3,256,256]{2,1,0:T(8,128)(2,1)}, bf16[3,256,256]{2,1,0:T(8,128)(2,1)S(1)}, u32[]{:S(2)}, u32[]{:S(2)}) collective-permute-start(bf16[3,256,256]{2,1,0:T(8,128)(2,1)} %get-tuple-element.1241), channel_id=1, source_target_pairs={{0,28},{4,0},{8,4},{12,8},{16,12},{20,16},{24,20},{28,24},{1,29},{... | collective-permute-start | bytes 1179656 | tf_op jit(solution)/shard_map/while/body/eval_jaxpr/ppermute | solution.py:19
  218.1 19.6 %collective-permute-start.15 = (bf16[3,256,256]{2,1,0:T(8,128)(2,1)S(1)}, bf16[3,256,256]{2,1,0:T(8,128)(2,1)}, u32[]{:S(2)}, u32[]{:S(2)}) collective-permute-start(bf16[3,256,256]{2,1,0:T(8,128)(2,1)S(1)} %get-tuple-element.1239), channel_id=1, source_target_pairs={{0,3},{1,0},{2,1},{3,2},{4,7},{5,4},{6,5},{7,6},{8,11},{9,8},{10,9... | collective-permute-start | bytes 1179656 | tf_op jit(solution)/shard_map/while/body/eval_jaxpr/ppermute | solution.py:19
  240.5 23.9 %collective-permute-start.8 = (bf16[3,256,256]{2,1,0:T(8,128)(2,1)S(1)}, bf16[3,256,256]{2,1,0:T(8,128)(2,1)S(1)}, u32[]{:S(2)}, u32[]{:S(2)}) collective-permute-start(bf16[3,256,256]{2,1,0:T(8,128)(2,1)S(1)} %get-tuple-element.1248), channel_id=1, source_target_pairs={{0,4},{4,8},{8,12},{12,16},{16,20},{20,24},{24,28},{28,0},{1,5},{5... | collective-permute-start | bytes 1179656 | tf_op jit(solution)/shard_map/while/body/eval_jaxpr/ppermute | solution.py:19
  242.9 17.9 %collective-permute-start.9 = (bf16[3]{0:T(256)(128)(2,1)S(1)}, bf16[3]{0:T(256)(128)(2,1)S(1)}, u32[]{:S(2)}, u32[]{:S(2)}) collective-permute-start(bf16[3]{0:T(256)(128)(2,1)S(1)} %get-tuple-element.1242), channel_id=1, source_target_pairs={{0,28},{4,0},{8,4},{12,8},{16,12},{20,16},{24,20},{28,24},{1,29},{... | collective-permute-start | bytes 26 | tf_op jit(solution)/shard_map/while/body/eval_jaxpr/ppermute | solution.py:19
  244.7 9.2 %collective-permute-start.10 = (bf16[3]{0:T(256)(128)(2,1)S(1)}, bf16[3]{0:T(256)(128)(2,1)S(1)}, u32[]{:S(2)}, u32[]{:S(2)}) collective-permute-start(bf16[3]{0:T(256)(128)(2,1)S(1)} %get-tuple-element.1249), channel_id=1, source_target_pairs={{0,4},{4,8},{8,12},{12,16},{16,20},{20,24},{24,28},{28,0},{1,5},{5... | collective-permute-start | bytes 26 | tf_op jit(solution)/shard_map/while/body/eval_jaxpr/ppermute | solution.py:19
  244.7 3.3 collective-permute-start.11
  248.0 21.7 %collective-permute-start.13 = (bf16[3,256,256]{2,1,0:T(8,128)(2,1)}, bf16[3,256,256]{2,1,0:T(8,128)(2,1)}, u32[]{:S(2)}, u32[]{:S(2)}) collective-permute-start(bf16[3,256,256]{2,1,0:T(8,128)(2,1)} %get-tuple-element.1246), channel_id=1, source_target_pairs={{0,1},{1,2},{2,3},{3,0},{4,5},{5,6},{6,7},{7,4},{8,9},{9,10},{10,1... | collective-permute-start | bytes 1179656 | tf_op jit(solution)/shard_map/while/body/eval_jaxpr/ppermute | solution.py:19
  248.0 19.4 %collective-permute-start.14 = (bf16[3,256,256]{2,1,0:T(8,128)(2,1)}, bf16[3,256,256]{2,1,0:T(8,128)(2,1)S(1)}, u32[]{:S(2)}, u32[]{:S(2)}) collective-permute-start(bf16[3,256,256]{2,1,0:T(8,128)(2,1)} %get-tuple-element.1241), channel_id=1, source_target_pairs={{0,28},{4,0},{8,4},{12,8},{16,12},{20,16},{24,20},{28,24},{1,29},{... | collective-permute-start | bytes 1179656 | tf_op jit(solution)/shard_map/while/body/eval_jaxpr/ppermute | solution.py:19
  253.9 19.2 %collective-permute-start.15 = (bf16[3,256,256]{2,1,0:T(8,128)(2,1)S(1)}, bf16[3,256,256]{2,1,0:T(8,128)(2,1)}, u32[]{:S(2)}, u32[]{:S(2)}) collective-permute-start(bf16[3,256,256]{2,1,0:T(8,128)(2,1)S(1)} %get-tuple-element.1239), channel_id=1, source_target_pairs={{0,3},{1,0},{2,1},{3,2},{4,7},{5,4},{6,5},{7,6},{8,11},{9,8},{10,9... | collective-permute-start | bytes 1179656 | tf_op jit(solution)/shard_map/while/body/eval_jaxpr/ppermute | solution.py:19
  276.1 23.7 %collective-permute-start.8 = (bf16[3,256,256]{2,1,0:T(8,128)(2,1)S(1)}, bf16[3,256,256]{2,1,0:T(8,128)(2,1)S(1)}, u32[]{:S(2)}, u32[]{:S(2)}) collective-permute-start(bf16[3,256,256]{2,1,0:T(8,128)(2,1)S(1)} %get-tuple-element.1248), channel_id=1, source_target_pairs={{0,4},{4,8},{8,12},{12,16},{16,20},{20,24},{24,28},{28,0},{1,5},{5... | collective-permute-start | bytes 1179656 | tf_op jit(solution)/shard_map/while/body/eval_jaxpr/ppermute | solution.py:19
  278.2 17.9 %collective-permute-start.9 = (bf16[3]{0:T(256)(128)(2,1)S(1)}, bf16[3]{0:T(256)(128)(2,1)S(1)}, u32[]{:S(2)}, u32[]{:S(2)}) collective-permute-start(bf16[3]{0:T(256)(128)(2,1)S(1)} %get-tuple-element.1242), channel_id=1, source_target_pairs={{0,28},{4,0},{8,4},{12,8},{16,12},{20,16},{24,20},{28,24},{1,29},{... | collective-permute-start | bytes 26 | tf_op jit(solution)/shard_map/while/body/eval_jaxpr/ppermute | solution.py:19
  280.3 9.2 %collective-permute-start.10 = (bf16[3]{0:T(256)(128)(2,1)S(1)}, bf16[3]{0:T(256)(128)(2,1)S(1)}, u32[]{:S(2)}, u32[]{:S(2)}) collective-permute-start(bf16[3]{0:T(256)(128)(2,1)S(1)} %get-tuple-element.1249), channel_id=1, source_target_pairs={{0,4},{4,8},{8,12},{12,16},{16,20},{20,24},{24,28},{28,0},{1,5},{5... | collective-permute-start | bytes 26 | tf_op jit(solution)/shard_map/while/body/eval_jaxpr/ppermute | solution.py:19
  280.3 3.3 collective-permute-start.11
  283.6 21.5 %collective-permute-start.13 = (bf16[3,256,256]{2,1,0:T(8,128)(2,1)}, bf16[3,256,256]{2,1,0:T(8,128)(2,1)}, u32[]{:S(2)}, u32[]{:S(2)}) collective-permute-start(bf16[3,256,256]{2,1,0:T(8,128)(2,1)} %get-tuple-element.1246), channel_id=1, source_target_pairs={{0,1},{1,2},{2,3},{3,0},{4,5},{5,6},{6,7},{7,4},{8,9},{9,10},{10,1... | collective-permute-start | bytes 1179656 | tf_op jit(solution)/shard_map/while/body/eval_jaxpr/ppermute | solution.py:19
  283.6 19.3 %collective-permute-start.14 = (bf16[3,256,256]{2,1,0:T(8,128)(2,1)}, bf16[3,256,256]{2,1,0:T(8,128)(2,1)S(1)}, u32[]{:S(2)}, u32[]{:S(2)}) collective-permute-start(bf16[3,256,256]{2,1,0:T(8,128)(2,1)} %get-tuple-element.1241), channel_id=1, source_target_pairs={{0,28},{4,0},{8,4},{12,8},{16,12},{20,16},{24,20},{28,24},{1,29},{... | collective-permute-start | bytes 1179656 | tf_op jit(solution)/shard_map/while/body/eval_jaxpr/ppermute | solution.py:19
  289.5 19.0 %collective-permute-start.15 = (bf16[3,256,256]{2,1,0:T(8,128)(2,1)S(1)}, bf16[3,256,256]{2,1,0:T(8,128)(2,1)}, u32[]{:S(2)}, u32[]{:S(2)}) collective-permute-start(bf16[3,256,256]{2,1,0:T(8,128)(2,1)S(1)} %get-tuple-element.1239), channel_id=1, source_target_pairs={{0,3},{1,0},{2,1},{3,2},{4,7},{5,4},{6,5},{7,6},{8,11},{9,8},{10,9... | collective-permute-start | bytes 1179656 | tf_op jit(solution)/shard_map/while/body/eval_jaxpr/ppermute | solution.py:19
  311.4 14.7 %collective-permute-start.32 = (bf16[3,256,256]{2,1,0:T(8,128)(2,1)}, bf16[3,256,256]{2,1,0:T(8,128)(2,1)S(1)}, u32[]{:S(2)}, u32[]{:S(2)}) collective-permute-start(bf16[3,256,256]{2,1,0:T(8,128)(2,1)} %get-tuple-element.591), channel_id=1, source_target_pairs={{0,28},{4,0},{8,4},{12,8},{16,12},{20,16},{24,20},{28,24},{1,29},{... | collective-permute-start | bytes 1179656 | tf_op jit(solution)/shard_map/ppermute | solution.py:19
  311.4 12.0 %collective-permute-start.34 = (bf16[3]{0:T(256)(128)(2,1)S(1)}, bf16[3]{0:T(256)(128)(2,1)S(1)}, u32[]{:S(2)}, u32[]{:S(2)}) collective-permute-start(bf16[3]{0:T(256)(128)(2,1)S(1)} %get-tuple-element.594), channel_id=1, source_target_pairs={{0,28},{4,0},{8,4},{12,8},{16,12},{20,16},{24,20},{28,24},{1,29},{... | collective-permute-start | bytes 26 | tf_op jit(solution)/shard_map/ppermute | solution.py:19
  311.4 12.7 %collective-permute-start.33 = (bf16[3]{0:T(256)(128)(2,1)S(1)}, bf16[3]{0:T(256)(128)(2,1)S(1)}, u32[]{:S(2)}, u32[]{:S(2)}) collective-permute-start(bf16[3]{0:T(256)(128)(2,1)S(1)} %get-tuple-element.593), channel_id=1, source_target_pairs={{0,3},{1,0},{2,1},{3,2},{4,7},{5,4},{6,5},{7,6},{8,11},{9,8},{10,9... | collective-permute-start | bytes 26 | tf_op jit(solution)/shard_map/ppermute | solution.py:19
  311.5 16.1 %collective-permute-start.35 = (bf16[3,256,256]{2,1,0:T(8,128)(2,1)S(1)}, bf16[3,256,256]{2,1,0:T(8,128)(2,1)S(1)}, u32[]{:S(2)}, u32[]{:S(2)}) collective-permute-start(bf16[3,256,256]{2,1,0:T(8,128)(2,1)S(1)} %get-tuple-element.597), channel_id=1, source_target_pairs={{0,3},{1,0},{2,1},{3,2},{4,7},{5,4},{6,5},{7,6},{8,11},{9,8},{10,9... | collective-permute-start | bytes 1179656 | tf_op jit(solution)/shard_map/ppermute | solution.py:19
  (48 other events, 186.9 us)
where the time goes:
time: 332 us; the launch traced here: 330 us
  starting transfers between devices  123 us (37%)
  waiting for transfers between devices  70.3 us (21%)
  other arithmetic  60.8 us (18%)
  local copies, waits for them, and re-layouts  56.5 us (17%)
  matrix products  18.2 us (5%)
    ppermute x68, starting transfers between devices, shifted(): lax.ppermute(shard, axis, [(i, (i + by) % length) for i in range(length)])  123 us
    ppermute x68, waiting for transfers between devices, shifted(): lax.ppermute(shard, axis, [(i, (i + by) % length) for i in range(length)])  70.3 us
    while x84, local copies, waits for them, and re-layouts  18.3 us
    dot_general x16, matrix products, contribution(): jnp.einsum('ixy,siyz->sxz', left_tiles, picked, preferred_element_type=jn...  17.2 us
    reshape x14, local copies, waits for them, and re-layouts, contribution(): picked.reshape(slot_count, slot_count, side, side)  15.3 us
    select_n x20, other arithmetic, choose(): jnp.where(flag, first, second)  15.1 us
    select_n x30, other arithmetic, contribution(): jnp.take(right_tiles, index.reshape(slot_count * slot_count), axis=0)  10.2 us
    unnamed x40, local copies, waits for them, and re-layouts  10.2 us
  transfers between devices with their start and end apart: 68, of which 21 were waited for; matrix products, arithmetic and copies ran while one was open for 31% of the time, Pallas kernels for 0%

commit v1 on v0

v1 whole, which is shorter than its diff:
```python
import functools

import jax
import jax.numpy as jnp
from jax import lax
from jax.experimental import pallas as pl
from jax.experimental.pallas import tpu as pltpu
from jax.sharding import PartitionSpec as P

MESH = pl.DeviceIdType.MESH
VMEM = pl.BlockSpec(memory_space=pltpu.VMEM)
SMEM = pl.BlockSpec(memory_space=pltpu.SMEM)


def send(src, dst, send_sem, recv_sem, row, col):
    return pltpu.make_async_remote_copy(
        src_ref=src,
        dst_ref=dst,
        send_sem=send_sem,
        recv_sem=recv_sem,
        device_id=(row, col),
        device_id_type=MESH,
    )


def greet(row_size, col_size, row, col, with_rows):
    barrier = pltpu.get_barrier_semaphore()
    count = col_size - 1
    for step in range(1, col_size):
        peer = lax.rem(col + step, col_size)
        pl.semaphore_signal(barrier, inc=1, device_id=(row, peer), device_id_type=MESH)
    if with_rows:
        count += row_size - 1
        for step in range(1, row_size):
            peer = lax.rem(row + step, row_size)
            pl.semaphore_signal(barrier, inc=1, device_id=(peer, col), device_id_type=MESH)
    pl.semaphore_wait(barrier, count)


class ColGather:
    def __init__(self, row, col, col_size, slots, own, panel, sems):
        self.row, self.col, self.slots = row, col, slots
        self.own, self.panel, self.sems = own, panel, sems
        self.chips = col_size // 2
        self.chip, self.core = col // 2, lax.rem(col, 2)
        self.partner = col + 1 - 2 * self.core

    def across(self, step, slot):
        target = 2 * lax.rem(self.chip + step, self.chips) + self.core
        return send(
            self.own.at[slot], self.panel.at[self.col, slot],
            self.sems.at[0, step - 1, slot], self.sems.at[1, step - 1, slot], self.row, target,
        )

    def beside(self, step, slot):
        origin = 2 * lax.rem(self.chip + self.chips - step, self.chips) + self.core
        src = self.own.at[slot] if step == 0 else self.panel.at[origin, slot]
        return send(
            src, self.panel.at[origin, slot],
            self.sems.at[2, step, slot], self.sems.at[3, step, slot], self.row, self.partner,
        )

    def start(self):
        for slot in range(self.slots):
            for step in range(1, self.chips):
                self.across(step, slot).start()
        for slot in range(self.slots):
            self.beside(0, slot).start()

    def forward(self):
        for slot in range(self.slots):
            for step in range(1, self.chips):
                self.across(step, slot).wait_recv()
                self.beside(step, slot).start()

    def finish(self):
        for step in range(self.chips):
            for slot in range(self.slots):
                if step:
                    self.across(step, slot).wait_send()
                self.beside(step, slot).wait()


def gather_kernel(
    row_size, col_size, tiles, ids, left, right, left_ids, right_ids,
    ids_out, col_sems, line_sems, side_sems, row_id_sems, col_id_sems,
):
    row, col = lax.axis_index("row"), lax.axis_index("col")
    slots, side = tiles.shape[0], tiles.shape[1]
    half = side // 2
    length = row_size // 2
    place, lane = row // 2, lax.rem(row, 2)
    mate = row + 1 - 2 * lane

    lane_iota = lax.broadcasted_iota(jnp.int32, (8, 128), 1)
    packed = jnp.full((8, 128), -1, jnp.int32)
    for slot in range(slots):
        packed = jnp.where(lane_iota == slot, ids[0, slot], packed)
    ids_out[...] = packed
    greet(row_size, col_size, row, col, True)

    pieces = [(slot, 0, side, False) for slot in range(slots - 1)]
    pieces += [(slots - 1, half, half, False)]
    early = (slots - 1, 0, half, True)
    mine = [early] + pieces
    count = len(mine)

    def view(ref, piece, origin=None):
        slot, first, rows, _ = piece
        if origin is None:
            return ref.at[slot, pl.ds(first, rows)]
        return ref.at[origin, slot, pl.ds(first, rows)]

    def to_mate(index, at):
        piece = mine[index]
        origin = 2 * at + lane
        return send(
            view(right, piece, origin), view(right, piece, origin),
            side_sems.at[0, at, index], side_sems.at[1, at, index], mate, col,
        )

    def own_to_mate(index):
        piece = mine[index]
        return send(
            view(tiles, piece), view(right, piece, row),
            side_sems.at[0, place, index], side_sems.at[1, place, index], mate, col,
        )

    def from_mate(index, at):
        piece = mine[index]
        origin = 2 * at + 1 - lane
        return send(
            view(right, piece, origin), view(right, piece, origin),
            side_sems.at[0, at, index], side_sems.at[1, at, index], mate, col,
        )

    def along(way, step, index, first=False):
        heading = 1 if way == 0 else -1
        piece = mine[0] if index == count else mine[index]
        on_lane = 1 - lane if index == count else lane
        origin = 2 * (place - heading * step) + on_lane
        src = view(tiles, piece) if first and index < count else view(right, piece, origin)
        return send(
            src, view(right, piece, origin),
            line_sems.at[way, 0, step, index], line_sems.at[way, 1, step, index],
            row + 2 * heading, col,
        )

    def landing(way, step, index):
        heading = 1 if way == 0 else -1
        piece = mine[0] if index == count else mine[index]
        on_lane = 1 - lane if index == count else lane
        origin = 2 * (place - heading * (step + 1)) + on_lane
        return send(
            view(right, piece, origin), view(right, piece, origin),
            line_sems.at[way, 0, step, index], line_sems.at[way, 1, step, index],
            row + 2 * heading, col,
        )

    can_send = (place + 1 < length, place > 0)

    def arrives(way, step):
        return place - step >= 1 if way == 0 else place + step + 1 < length

    def goes(way, step):
        if way == 0:
            return (place - step >= 0) & (place + 1 < length)
        return (place + step < length) & (place > 0)

    own_to_mate(0).start()
    for index in range(count):
        for way in range(2):
            @pl.when(can_send[way])
            def _():
                along(way, 0, index, True).start()
        if index:
            own_to_mate(index).start()
    left_gather = ColGather(row, col, col_size, slots, tiles, left, col_sems)
    left_gather.start()

    def id_row(step):
        return send(
            ids_out, right_ids.at[row], row_id_sems.at[0, step], row_id_sems.at[1, step],
            lax.rem(row + step, row_size), col,
        )

    def id_col(step):
        return send(
            ids_out, left_ids.at[col], col_id_sems.at[0, step], col_id_sems.at[1, step],
            row, lax.rem(col + step, col_size),
        )

    for step in range(1, row_size):
        id_row(step).start()
    for step in range(1, col_size):
        id_col(step).start()

    from_mate(0, place).wait_recv()
    for way in range(2):
        @pl.when(can_send[way])
        def _():
            along(way, 0, count).start()

    right[row] = tiles[...]
    left[col] = tiles[...]
    right_ids[row] = packed
    left_ids[col] = packed

    def turn(step, unused):
        for index in list(range(count)) + [count]:
            for way in range(2):
                @pl.when(arrives(way, step))
                def _():
                    landing(way, step, index).wait_recv()

                    @pl.when(can_send[way])
                    def _():
                        along(way, step + 1, index).start()

                    if 0 < index < count:
                        heading = 1 if way == 0 else -1
                        to_mate(index, place - heading * (step + 1)).start()
        return unused

    turn(0, 0)
    left_gather.forward()
    lax.fori_loop(1, length - 1, turn, 0)

    left_gather.finish()
    for step in range(1, row_size):
        id_row(step).wait()
    for step in range(1, col_size):
        id_col(step).wait()

    def settle(step, unused):
        for index in range(count + 1):
            for way in range(2):
                @pl.when(goes(way, step))
                def _():
                    along(way, step, index).wait_send()
        return unused

    lax.fori_loop(0, length - 1, settle, 0)
    own_to_mate(0).wait_send()

    def collect(at, unused):
        for index in range(1, count):
            to_mate(index, at).wait_send()
            from_mate(index, at).wait_recv()
        return unused

    lax.fori_loop(0, length, collect, 0)


def squares_kernel(row_size, col_size, square, panel, col_sems):
    row, col = lax.axis_index("row"), lax.axis_index("col")
    greet(row_size, col_size, row, col, False)
    gather = ColGather(row, col, col_size, square.shape[0], square, panel, col_sems)
    gather.start()
    panel[col] = square[...]
    gather.forward()
    gather.finish()


def products(row_size, col_size, left, right, left_ids, right_ids, mask, total):
    row, col = lax.axis_index("row"), lax.axis_index("col")
    slots = total.shape[0]
    block_rows, block_cols = mask.shape[0] // row_size, mask.shape[1] // col_size
    total[...] = jnp.zeros_like(total)
    for slot in range(slots):
        own = left_ids[col, 0, slot]
        own_row = own // block_cols
        out_row = row * block_rows + own_row
        out_col = col * block_cols + lax.rem(own, block_cols)
        live = mask[out_row, out_col] > 0

        @pl.when(live)
        def _():
            def panel_step(region, unused):
                for place in range(slots):
                    label = left_ids[region, 0, place]
                    inner = region * block_cols + lax.rem(label, block_cols)
                    use = (label // block_cols == own_row) & (mask[out_row, inner] > 0)
                    use = use & (mask[inner, out_col] > 0)

                    @pl.when(use)
                    def _():
                        band = inner // block_rows
                        wanted = lax.rem(inner, block_rows) * block_cols + lax.rem(own, block_cols)
                        spot = jnp.int32(0)
                        for other in range(1, slots):
                            spot = jnp.where(right_ids[band, 0, other] == wanted, other, spot)
                        total[slot] += jnp.dot(
                            left[region, place], right[band, spot], preferred_element_type=jnp.float32
                        )
                return unused

            lax.fori_loop(0, col_size, panel_step, 0)


def square_kernel(row_size, col_size, left, right, left_ids, right_ids, mask, out, total):
    products(row_size, col_size, left, right, left_ids, right_ids, mask, total)
    out[...] = total[...].astype(out.dtype)


def cube_kernel(row_size, col_size, square, right, left_ids, right_ids, mask, out, total):
    products(row_size, col_size, square, right, left_ids, right_ids, mask, total)
    col = lax.axis_index("col")
    out[...] = (3.0 * square[col].astype(jnp.float32) - 2.0 * total[...]).astype(out.dtype)


def solution(mesh):
    row_size, col_size = mesh.shape["row"], mesh.shape["col"]
    length, chips = row_size // 2, col_size // 2
    dma = pltpu.SemaphoreType.DMA

    def local(tiles, stack_index, block_mask):
        stack, ids = tiles[0, 0], stack_index[0]
        slots, side, _ = stack.shape
        shape = jax.ShapeDtypeStruct
        col_sems = dma((4, chips, slots))
        left, right, left_ids, right_ids = pl.pallas_call(
            functools.partial(gather_kernel, row_size, col_size),
            out_shape=(
                shape((col_size, slots, side, side), stack.dtype),
                shape((row_size, slots, side, side), stack.dtype),
                shape((col_size, 8, 128), jnp.int32),
                shape((row_size, 8, 128), jnp.int32),
            ),
            in_specs=[VMEM, SMEM],
            out_specs=(VMEM,) * 4,
            scratch_shapes=[
                pltpu.VMEM((8, 128), jnp.int32),
                col_sems,
                dma((2, 2, length, slots + 2)),
                dma((2, length, slots + 1)),
                dma((2, row_size)),
                dma((2, col_size)),
            ],
            compiler_params=pltpu.CompilerParams(collective_id=0, has_side_effects=True),
            name="gather",
        )(stack, ids)
        square = pl.pallas_call(
            functools.partial(square_kernel, row_size, col_size),
            out_shape=shape(stack.shape, stack.dtype),
            in_specs=[VMEM, VMEM, SMEM, SMEM, SMEM],
            out_specs=VMEM,
            scratch_shapes=[pltpu.VMEM(stack.shape, jnp.float32)],
            name="square",
        )(left, right, left_ids, right_ids, block_mask)
        squares = pl.pallas_call(
            functools.partial(squares_kernel, row_size, col_size),
            out_shape=shape((col_size, slots, side, side), stack.dtype),
            in_specs=[VMEM],
            out_specs=VMEM,
            scratch_shapes=[col_sems],
            compiler_params=pltpu.CompilerParams(collective_id=1, has_side_effects=True),
            name="squares",
        )(square)
        purified = pl.pallas_call(
            functools.partial(cube_kernel, row_size, col_size),
            out_shape=shape(stack.shape, stack.dtype),
            in_specs=[VMEM, VMEM, SMEM, SMEM, SMEM],
            out_specs=VMEM,
            scratch_shapes=[pltpu.VMEM(stack.shape, jnp.float32)],
            name="cube",
        )(squares, right, left_ids, right_ids, block_mask)
        return purified[None, None]

    placed = (P("row", "col", None, None, None), P("row", "col", None), P())
    return jax.shard_map(
        local,
        mesh=mesh,
        in_specs=placed,
        out_specs=P("row", "col", None, None, None),
        check_vma=False,
    )
```

time: 332 us -> 68.7 us (0.21)
  starting transfers between devices: 123 us -> 0 us
  waiting for transfers between devices: 70.3 us -> 0 us
  Pallas kernels: 0 us -> 67.9 us
  other arithmetic: 60.8 us -> 0 us
  local copies, waits for them, and re-layouts: 56.5 us -> 0 us
  matrix products: 18.2 us -> 0 us
    ppermute x68 -> x0, starting transfers between devices: 123 us -> none  [shifted(): lax.ppermute(shard, axis, [(i, (i + by) % length) for i in range(length)])]
    ppermute x68 -> x0, waiting for transfers between devices: 70.3 us -> none  [shifted(): lax.ppermute(shard, axis, [(i, (i + by) % length) for i in range(length)])]
    pallas_call x0 -> x4, Pallas kernels: none -> 67.9 us  [the longest x1 43 us: local(): pl.pallas_call(functools.partial(gather_kernel, row_size, col_size), out_...]
    select_n x72 -> x0, other arithmetic: 31.9 us -> none  [the longest x20 15.1 us: choose(): jnp.where(flag, first, second)]
    while x87 -> x0, local copies, waits for them, and re-layouts: 19.6 us -> none
    dot_general x17 -> x0, matrix products: 18.2 us -> none  [the longest x16 17.2 us: contribution(): jnp.einsum('ixy,siyz->sxz', left_tiles, picked, preferred_element_type=jn...]
    reshape x29 -> x0, local copies, waits for them, and re-layouts: 16.5 us -> none  [the longest x14 15.3 us: contribution(): picked.reshape(slot_count, slot_count, side, side)]
    unnamed x40 -> x0, local copies, waits for them, and re-layouts: 10.2 us -> none
  transfers between devices with their start and end apart: 68 -> 0, of which waited for: 21 -> 0; matrix products, arithmetic and copies ran while one was open for 31% -> 0% of each run, Pallas kernels for 0% -> 0%
where the time goes in v1:
time: 68.7 us; the launch traced here: 67.9 us
  Pallas kernels  67.9 us (99%)
    pallas_call x1, Pallas kernels, local(): pl.pallas_call(functools.partial(gather_kernel, row_size, col_size), out_...  43 us
    pallas_call x1, Pallas kernels, local(): pl.pallas_call(functools.partial(squares_kernel, row_size, col_size), out...  16.3 us
    pallas_call x1, Pallas kernels, local(): pl.pallas_call(functools.partial(cube_kernel, row_size, col_size), out_sh...  4.32 us
    pallas_call x1, Pallas kernels, local(): pl.pallas_call(functools.partial(square_kernel, row_size, col_size), out_...  4.24 us

profile of v1, /device:TPU:1, one launch (start us, length us, event | category | flops | bytes accessed | tf_op | source)
XLA Modules:
  0.0 67.9 jit_solution(6083888529042800696)
XLA Ops:
  0.0 43.0 %gather.1 = (bf16[4,3,256,256]{3,2,1,0:T(8,128)(2,1)}, bf16[8,3,256,256]{3,2,1,0:T(8,128)(2,1)}, s32[4,8,128]{2,1,0:T(8,128)}, s32[8,8,128]{2,1,0:T(8,128)}) custom-call(bf16[3,256,256]{2,1,0:T(8,128)(2,1)} %bitcast.3, s32[1,3]{1,0:T(1,128)} %bitcast.4), custom_call_target="tpu_custom_call" | custom-call | tf_op jit(solution)/shard_map/gather/pallas_call | solution.py:322
  43.0 4.2 %square.1 = bf16[3,256,256]{2,1,0:T(8,128)(2,1)} custom-call(bf16[4,3,256,256]{3,2,1,0:T(8,128)(2,1)} %get-tuple-element.9.left, bf16[8,3,256,256]{3,2,1,0:T(8,128)(2,1)} %get-tuple-element.10.right, s32[4,8,128]{2,1,0:T(8,128)} %get-tuple-element.11.left_ids, s32[8,8,128]{2,1,0:T(8,128)} %get-tuple-element.12.right_ids, s32[64,64]{1,0:T(8,128)} %mask.3), custom_call_target="tpu_custom_call" | custom-call | tf_op jit(solution)/shard_map/square/pallas_call | solution.py:343
  47.3 16.3 %squares.1.square = bf16[4,3,256,256]{3,2,1,0:T(8,128)(2,1)} custom-call(bf16[3,256,256]{2,1,0:T(8,128)(2,1)} %square.1), custom_call_target="tpu_custom_call" | custom-call | tf_op jit(solution)/shard_map/squares/pallas_call | solution.py:351
  63.5 4.3 %cube.1 = bf16[3,256,256]{2,1,0:T(8,128)(2,1)} custom-call(bf16[4,3,256,256]{3,2,1,0:T(8,128)(2,1)} %squares.1.square, bf16[8,3,256,256]{3,2,1,0:T(8,128)(2,1)} %get-tuple-element.10.right, s32[4,8,128]{2,1,0:T(8,128)} %get-tuple-element.11.left_ids, s32[8,8,128]{2,1,0:T(8,128)} %get-tuple-element.12.right_ids, s32[64,64]{1,0:T(8,128)} %mask.3), custom_call_target="tpu_custom_call" | custom-call | tf_op jit(solution)/shard_map/cube/pallas_call | solution.py:360

commit v2 on v1

--- a/solution.py
+++ b/solution.py
@@ -67,23 +67,35 @@
         for slot in range(self.slots):
             self.beside(0, slot).start()
 
-    def forward(self):
+    def origin(self, step, core):
+        return 2 * lax.rem(self.chip + self.chips - step, self.chips) + core
+
+    def forward(self, use=None):
         for slot in range(self.slots):
             for step in range(1, self.chips):
                 self.across(step, slot).wait_recv()
                 self.beside(step, slot).start()
-
-    def finish(self):
+                if use is not None:
+                    use(self.origin(step, self.core), slot)
+
+    def collect(self, use, steps):
+        for step in steps:
+            for slot in range(self.slots):
+                self.beside(step, slot).wait_recv()
+                if use is not None:
+                    use(self.origin(step, 1 - self.core), slot)
+
+    def settle(self):
         for step in range(self.chips):
             for slot in range(self.slots):
                 if step:
                     self.across(step, slot).wait_send()
-                self.beside(step, slot).wait()
-
-
-def gather_kernel(
-    row_size, col_size, tiles, ids, left, right, left_ids, right_ids,
-    ids_out, col_sems, line_sems, side_sems, row_id_sems, col_id_sems,
+                self.beside(step, slot).wait_send()
+
+
+def kernel(
+    row_size, col_size, tiles, ids, mask, out, left, right, squares, square, total, left_ids, right_ids, ids_out,
+    left_labels, right_labels, col_sems, square_sems, line_sems, side_sems, row_id_sems, col_id_sems, label_sems,
 ):
     row, col = lax.axis_index("row"), lax.axis_index("col")
     slots, side = tiles.shape[0], tiles.shape[1]
@@ -222,15 +234,119 @@
                         to_mate(index, place - heading * (step + 1)).start()
         return unused
 
-    turn(0, 0)
-    left_gather.forward()
-    lax.fori_loop(1, length - 1, turn, 0)
-
-    left_gather.finish()
+    block_rows, block_cols = mask.shape[0] // row_size, mask.shape[1] // col_size
+    owns = []
+    for slot in range(slots):
+        own = ids[0, slot]
+        own_row, own_col = own // block_cols, lax.rem(own, block_cols)
+        out_row, out_col = row * block_rows + own_row, col * block_cols + own_col
+        owns.append((own_row, own_col, out_row, out_col, mask[out_row, out_col] > 0))
+
+    def find(labels, region, wanted):
+        spot, found = jnp.int32(0), labels[region, 0, 0] == wanted
+        for other in range(1, slots):
+            same = labels[region, 0, other] == wanted
+            spot = jnp.where(same, other, spot)
+            found = found | same
+        return spot, found
+
+    def square_term(origin, place):
+        label = right_labels[origin, 0, place]
+        inner = origin * block_rows + label // block_cols
+        band = inner // block_cols
+        chosen = []
+        for own_row, own_col, out_row, out_col, live in owns:
+            spot, found = find(left_labels, band, own_row * block_cols + lax.rem(inner, block_cols))
+            use = live & found & (lax.rem(label, block_cols) == own_col)
+            use = use & (mask[out_row, inner] > 0) & (mask[inner, out_col] > 0)
+            tile = left[band, spot]
+            chosen.append(jnp.where(use, tile, jnp.zeros_like(tile)))
+        term = jnp.dot(
+            jnp.concatenate(chosen, axis=0), right[origin, place], preferred_element_type=jnp.float32
+        )
+        total[...] += term.reshape(total.shape)
+
+    def cube_term(origin, place):
+        label = left_labels[origin, 0, place]
+        inner = origin * block_cols + lax.rem(label, block_cols)
+        band = inner // block_rows
+        piece = squares[origin, place]
+        for slot, (own_row, own_col, out_row, out_col, live) in enumerate(owns):
+            spot, found = find(right_labels, band, lax.rem(inner, block_rows) * block_cols + own_col)
+            use = live & found & (label // block_cols == own_row)
+            use = use & (mask[out_row, inner] > 0) & (mask[inner, out_col] > 0)
+            tile = right[band, spot]
+            total[slot] += jnp.dot(
+                piece, jnp.where(use, tile, jnp.zeros_like(tile)), preferred_element_type=jnp.float32
+            )
+
+    def stack_terms(origin, wait=None):
+        for slot in range(slots):
+            if wait is not None:
+                wait(slot)
+            square_term(origin, slot)
+
+    def mate_terms(at):
+        stack_terms(2 * at + 1 - lane, lambda slot: from_mate(slot + 1, at).wait_recv())
+
+    def consume(step):
+        for way in range(2):
+            @pl.when(arrives(way, step))
+            def _():
+                heading = 1 if way == 0 else -1
+                stack_terms(2 * (place - heading * (step + 1)) + lane)
+        for way in range(2):
+            @pl.when(arrives(way, step))
+            def _():
+                heading = 1 if way == 0 else -1
+                mate_terms(place - heading * (step + 1))
+
+    total[...] = jnp.zeros_like(total)
     for step in range(1, row_size):
         id_row(step).wait()
     for step in range(1, col_size):
         id_col(step).wait()
+    copies = (
+        pltpu.make_async_copy(left_ids, left_labels, label_sems.at[0]),
+        pltpu.make_async_copy(right_ids, right_labels, label_sems.at[1]),
+    )
+    for copy in copies:
+        copy.start()
+    for copy in copies:
+        copy.wait()
+    turn(0, 0)
+    left_gather.forward()
+    left_gather.collect(None, range(left_gather.chips))
+    stack_terms(row)
+    mate_terms(place)
+
+    def advance(step, unused):
+        turn(step, 0)
+        consume(step - 1)
+        return unused
+
+    lax.fori_loop(1, length - 1, advance, 0)
+    consume(length - 2)
+
+    square[...] = total[...].astype(square.dtype)
+
+    def keep(slot, unused):
+        squares[col, slot] = square[slot]
+        return unused
+
+    lax.fori_loop(0, slots, keep, 0)
+    square_gather = ColGather(row, col, col_size, slots, square, squares, square_sems)
+    square_gather.start()
+    total[...] = jnp.zeros_like(total)
+    for slot in range(slots):
+        cube_term(col, slot)
+    square_gather.collect(cube_term, [0])
+    square_gather.forward(cube_term)
+    square_gather.collect(cube_term, range(1, square_gather.chips))
+    out[...] = (3.0 * square[...].astype(jnp.float32) - 2.0 * total[...]).astype(out.dtype)
+
+    left_gather.settle()
+    square_gather.settle()
 
     def settle(step, unused):
         for index in range(count + 1):
@@ -246,67 +362,9 @@
     def collect(at, unused):
         for index in range(1, count):
             to_mate(index, at).wait_send()
-            from_mate(index, at).wait_recv()
         return unused
 
     lax.fori_loop(0, length, collect, 0)
-
-
-def squares_kernel(row_size, col_size, square, panel, col_sems):
-    row, col = lax.axis_index("row"), lax.axis_index("col")
-    greet(row_size, col_size, row, col, False)
-    gather = ColGather(row, col, col_size, square.shape[0], square, panel, col_sems)
-    gather.start()
-    panel[col] = square[...]
-    gather.forward()
-    gather.finish()
-
-
-def products(row_size, col_size, left, right, left_ids, right_ids, mask, total):
-    row, col = lax.axis_index("row"), lax.axis_index("col")
-    slots = total.shape[0]
-    block_rows, block_cols = mask.shape[0] // row_size, mask.shape[1] // col_size
-    total[...] = jnp.zeros_like(total)
-    for slot in range(slots):
-        own = left_ids[col, 0, slot]
-        own_row = own // block_cols
-        out_row = row * block_rows + own_row
-        out_col = col * block_cols + lax.rem(own, block_cols)
-        live = mask[out_row, out_col] > 0
-
-        @pl.when(live)
-        def _():
-            def panel_step(region, unused):
-                for place in range(slots):
-                    label = left_ids[region, 0, place]
-                    inner = region * block_cols + lax.rem(label, block_cols)
-                    use = (label // block_cols == own_row) & (mask[out_row, inner] > 0)
-                    use = use & (mask[inner, out_col] > 0)
-
-                    @pl.when(use)
-                    def _():
-                        band = inner // block_rows
-                        wanted = lax.rem(inner, block_rows) * block_cols + lax.rem(own, block_cols)
-                        spot = jnp.int32(0)
-                        for other in range(1, slots):
-                            spot = jnp.where(right_ids[band, 0, other] == wanted, other, spot)
-                        total[slot] += jnp.dot(
-                            left[region, place], right[band, spot], preferred_element_type=jnp.float32
-                        )
-                return unused
-
-            lax.fori_loop(0, col_size, panel_step, 0)
-
-
-def square_kernel(row_size, col_size, left, right, left_ids, right_ids, mask, out, total):
-    products(row_size, col_size, left, right, left_ids, right_ids, mask, total)
-    out[...] = total[...].astype(out.dtype)
-
-
-def cube_kernel(row_size, col_size, square, right, left_ids, right_ids, mask, out, total):
-    products(row_size, col_size, square, right, left_ids, right_ids, mask, total)
-    col = lax.axis_index("col")
-    out[...] = (3.0 * square[col].astype(jnp.float32) - 2.0 * total[...]).astype(out.dtype)
 
 
 def solution(mesh):
@@ -317,54 +375,34 @@
     def local(tiles, stack_index, block_mask):
         stack, ids = tiles[0, 0], stack_index[0]
         slots, side, _ = stack.shape
-        shape = jax.ShapeDtypeStruct
-        col_sems = dma((4, chips, slots))
-        left, right, left_ids, right_ids = pl.pallas_call(
-            functools.partial(gather_kernel, row_size, col_size),
-            out_shape=(
-                shape((col_size, slots, side, side), stack.dtype),
-                shape((row_size, slots, side, side), stack.dtype),
-                shape((col_size, 8, 128), jnp.int32),
-                shape((row_size, 8, 128), jnp.int32),
-            ),
-            in_specs=[VMEM, SMEM],
-            out_specs=(VMEM,) * 4,
+        col_panel = pltpu.VMEM((col_size, slots, side, side), stack.dtype)
+        purified = pl.pallas_call(
+            functools.partial(kernel, row_size, col_size),
+            out_shape=jax.ShapeDtypeStruct(stack.shape, stack.dtype),
+            in_specs=[VMEM, SMEM, SMEM],
+            out_specs=VMEM,
             scratch_shapes=[
+                col_panel,
+                pltpu.VMEM((row_size, slots, side, side), stack.dtype),
+                col_panel,
+                pltpu.VMEM(stack.shape, stack.dtype),
+                pltpu.VMEM(stack.shape, jnp.float32),
+                pltpu.VMEM((col_size, 8, 128), jnp.int32),
+                pltpu.VMEM((row_size, 8, 128), jnp.int32),
                 pltpu.VMEM((8, 128), jnp.int32),
-                col_sems,
+                pltpu.SMEM((col_size, 8, 128), jnp.int32),
+                pltpu.SMEM((row_size, 8, 128), jnp.int32),
+                dma((4, chips, slots)),
+                dma((4, chips, slots)),
                 dma((2, 2, length, slots + 2)),
                 dma((2, length, slots + 1)),
                 dma((2, row_size)),
                 dma((2, col_size)),
+                dma((2,)),
             ],
             compiler_params=pltpu.CompilerParams(collective_id=0, has_side_effects=True),
-            name="gather",
-        )(stack, ids)
-        square = pl.pallas_call(
-            functools.partial(square_kernel, row_size, col_size),
-            out_shape=shape(stack.shape, stack.dtype),
-            in_specs=[VMEM, VMEM, SMEM, SMEM, SMEM],
-            out_specs=VMEM,
-            scratch_shapes=[pltpu.VMEM(stack.shape, jnp.float32)],
-            name="square",
-        )(left, right, left_ids, right_ids, block_mask)
-        squares = pl.pallas_call(
-            functools.partial(squares_kernel, row_size, col_size),
-            out_shape=shape((col_size, slots, side, side), stack.dtype),
-            in_specs=[VMEM],
-            out_specs=VMEM,
-            scratch_shapes=[col_sems],
-            compiler_params=pltpu.CompilerParams(collective_id=1, has_side_effects=True),
-            name="squares",
-        )(square)
-        purified = pl.pallas_call(
-            functools.partial(cube_kernel, row_size, col_size),
-            out_shape=shape(stack.shape, stack.dtype),
-            in_specs=[VMEM, VMEM, SMEM, SMEM, SMEM],
-            out_specs=VMEM,
-            scratch_shapes=[pltpu.VMEM(stack.shape, jnp.float32)],
-            name="cube",
-        )(squares, right, left_ids, right_ids, block_mask)
+            name="purify",
+        )(stack, ids, block_mask)
         return purified[None, None]
 
     placed = (P("row", "col", None, None, None), P("row", "col", None), P())

time: 68.7 us -> 56.8 us (0.83)
  Pallas kernels: 67.9 us -> 54.8 us
  local copies, waits for them, and re-layouts: 0 us -> 1.77 us
    pallas_call x4 -> x1, Pallas kernels: 67.9 us -> 54.8 us  [local(): pl.pallas_call(functools.partial(kernel, row_size, col_size), out_shape=j...]
    unnamed x0 -> x1, local copies, waits for them, and re-layouts: none -> 1.77 us
where the time goes in v2:
time: 56.8 us; the launch traced here: 56.6 us
  Pallas kernels  54.8 us (96%)
  local copies, waits for them, and re-layouts  1.77 us (3%)
    pallas_call x1, Pallas kernels, local(): pl.pallas_call(functools.partial(kernel, row_size, col_size), out_shape=j...  54.8 us
    unnamed x1, local copies, waits for them, and re-layouts  1.77 us

profile of v2, /device:TPU:1, one launch (start us, length us, event | category | flops | bytes accessed | tf_op | source)
XLA Modules:
  0.0 56.6 jit_solution(3183348626457322726)
XLA Ops:
  0.0 54.8 %purify.1 = bf16[3,256,256]{2,1,0:T(8,128)(2,1)} custom-call(bf16[3,256,256]{2,1,0:T(8,128)(2,1)} %bitcast.4, s32[1,3]{1,0:T(1,128)} %bitcast.5, s32[64,64]{1,0:T(8,128)} %mask.1), custom_call_target="tpu_custom_call" | custom-call | tf_op jit(solution)/shard_map/purify/pallas_call | solution.py:379
  54.8 1.8 %copy.5 = bf16[1,1,3,256,256]{4,3,2,1,0:T(8,128)(2,1)} copy(bf16[1,1,3,256,256]{4,3,2,1,0:T(8,128)(2,1)} %bitcast.3) | data formatting | bytes 786432

commit v3 on v2

--- a/solution.py
+++ b/solution.py
@@ -38,7 +38,8 @@
 
 
 class ColGather:
-    def __init__(self, row, col, col_size, slots, own, panel, sems):
+    def __init__(self, row, col, col_size, slots, own, panel, sems, part, start, width):
+        self.columns, self.part = pl.ds(start, width), 4 * part
         self.row, self.col, self.slots = row, col, slots
         self.own, self.panel, self.sems = own, panel, sems
         self.chips = col_size // 2
@@ -48,16 +49,19 @@
     def across(self, step, slot):
         target = 2 * lax.rem(self.chip + step, self.chips) + self.core
         return send(
-            self.own.at[slot], self.panel.at[self.col, slot],
-            self.sems.at[0, step - 1, slot], self.sems.at[1, step - 1, slot], self.row, target,
+            self.own.at[slot, :, self.columns], self.panel.at[self.col, slot, :, self.columns],
+            self.sems.at[self.part, step - 1, slot], self.sems.at[self.part + 1, step - 1, slot],
+            self.row, target,
         )
 
     def beside(self, step, slot):
         origin = 2 * lax.rem(self.chip + self.chips - step, self.chips) + self.core
-        src = self.own.at[slot] if step == 0 else self.panel.at[origin, slot]
-        return send(
-            src, self.panel.at[origin, slot],
-            self.sems.at[2, step, slot], self.sems.at[3, step, slot], self.row, self.partner,
+        panel = self.panel.at[origin, slot, :, self.columns]
+        src = self.own.at[slot, :, self.columns] if step == 0 else panel
+        return send(
+            src, panel,
+            self.sems.at[self.part + 2, step, slot], self.sems.at[self.part + 3, step, slot],
+            self.row, self.partner,
         )
 
     def start(self):
@@ -117,55 +121,56 @@
     mine = [early] + pieces
     count = len(mine)
 
-    def view(ref, piece, origin=None):
+    def view(ref, piece, part, origin=None):
         slot, first, rows, _ = piece
+        columns = pl.ds(part * half, half)
         if origin is None:
-            return ref.at[slot, pl.ds(first, rows)]
-        return ref.at[origin, slot, pl.ds(first, rows)]
-
-    def to_mate(index, at):
+            return ref.at[slot, pl.ds(first, rows), columns]
+        return ref.at[origin, slot, pl.ds(first, rows), columns]
+
+    def to_mate(index, at, part):
         piece = mine[index]
         origin = 2 * at + lane
         return send(
-            view(right, piece, origin), view(right, piece, origin),
-            side_sems.at[0, at, index], side_sems.at[1, at, index], mate, col,
-        )
-
-    def own_to_mate(index):
+            view(right, piece, part, origin), view(right, piece, part, origin),
+            side_sems.at[2 * part, at, index], side_sems.at[2 * part + 1, at, index], mate, col,
+        )
+
+    def own_to_mate(index, part):
         piece = mine[index]
         return send(
-            view(tiles, piece), view(right, piece, row),
-            side_sems.at[0, place, index], side_sems.at[1, place, index], mate, col,
-        )
-
-    def from_mate(index, at):
+            view(tiles, piece, part), view(right, piece, part, row),
+            side_sems.at[2 * part, place, index], side_sems.at[2 * part + 1, place, index], mate, col,
+        )
+
+    def from_mate(index, at, part):
         piece = mine[index]
         origin = 2 * at + 1 - lane
         return send(
-            view(right, piece, origin), view(right, piece, origin),
-            side_sems.at[0, at, index], side_sems.at[1, at, index], mate, col,
-        )
-
-    def along(way, step, index, first=False):
+            view(right, piece, part, origin), view(right, piece, part, origin),
+            side_sems.at[2 * part, at, index], side_sems.at[2 * part + 1, at, index], mate, col,
+        )
+
+    def along(way, step, index, part, first=False):
         heading = 1 if way == 0 else -1
         piece = mine[0] if index == count else mine[index]
         on_lane = 1 - lane if index == count else lane
         origin = 2 * (place - heading * step) + on_lane
-        src = view(tiles, piece) if first and index < count else view(right, piece, origin)
-        return send(
-            src, view(right, piece, origin),
-            line_sems.at[way, 0, step, index], line_sems.at[way, 1, step, index],
+        src = view(tiles, piece, part) if first and index < count else view(right, piece, part, origin)
+        return send(
+            src, view(right, piece, part, origin),
+            line_sems.at[2 * part + way, 0, step, index], line_sems.at[2 * part + way, 1, step, index],
             row + 2 * heading, col,
         )
 
-    def landing(way, step, index):
+    def landing(way, step, index, part):
         heading = 1 if way == 0 else -1
         piece = mine[0] if index == count else mine[index]
         on_lane = 1 - lane if index == count else lane
         origin = 2 * (place - heading * (step + 1)) + on_lane
         return send(
-            view(right, piece, origin), view(right, piece, origin),
-            line_sems.at[way, 0, step, index], line_sems.at[way, 1, step, index],
+            view(right, piece, part, origin), view(right, piece, part, origin),
+            line_sems.at[2 * part + way, 0, step, index], line_sems.at[2 * part + way, 1, step, index],
             row + 2 * heading, col,
         )
 
@@ -179,15 +184,25 @@
             return (place - step >= 0) & (place + 1 < length)
         return (place + step < length) & (place > 0)
 
-    own_to_mate(0).start()
-    for index in range(count):
+    def begin(part):
+        own_to_mate(0, part).start()
+        for index in range(count):
+            for way in range(2):
+                @pl.when(can_send[way])
+                def _():
+                    along(way, 0, index, part, True).start()
+            if index:
+                own_to_mate(index, part).start()
+
+    def begin_mate(part):
+        from_mate(0, place, part).wait_recv()
         for way in range(2):
             @pl.when(can_send[way])
             def _():
-                along(way, 0, index, True).start()
-        if index:
-            own_to_mate(index).start()
-    left_gather = ColGather(row, col, col_size, slots, tiles, left, col_sems)
+                along(way, 0, count, part).start()
+
+    begin(0)
+    left_gather = ColGather(row, col, col_size, slots, tiles, left, col_sems, 0, 0, side)
     left_gather.start()
 
     def id_row(step):
@@ -207,32 +222,27 @@
     for step in range(1, col_size):
         id_col(step).start()
 
-    from_mate(0, place).wait_recv()
-    for way in range(2):
-        @pl.when(can_send[way])
-        def _():
-            along(way, 0, count).start()
+    begin_mate(0)
 
     right[row] = tiles[...]
     left[col] = tiles[...]
     right_ids[row] = packed
     left_ids[col] = packed
 
-    def turn(step, unused):
+    def turn(step, part):
         for index in list(range(count)) + [count]:
             for way in range(2):
                 @pl.when(arrives(way, step))
                 def _():
-                    landing(way, step, index).wait_recv()
+                    landing(way, step, index, part).wait_recv()
 
                     @pl.when(can_send[way])
                     def _():
-                        along(way, step + 1, index).start()
+                        along(way, step + 1, index, part).start()
 
                     if 0 < index < count:
                         heading = 1 if way == 0 else -1
-                        to_mate(index, place - heading * (step + 1)).start()
-        return unused
+                        to_mate(index, place - heading * (step + 1), part).start()
 
     block_rows, block_cols = mask.shape[0] // row_size, mask.shape[1] // col_size
     owns = []
@@ -250,7 +260,7 @@
             found = found | same
         return spot, found
 
-    def square_term(origin, place):
+    def square_term(origin, place, part):
         label = right_labels[origin, 0, place]
         inner = origin * block_rows + label // block_cols
         band = inner // block_cols
@@ -262,44 +272,68 @@
             tile = left[band, spot]
             chosen.append(jnp.where(use, tile, jnp.zeros_like(tile)))
         term = jnp.dot(
-            jnp.concatenate(chosen, axis=0), right[origin, place], preferred_element_type=jnp.float32
-        )
-        total[...] += term.reshape(total.shape)
-
-    def cube_term(origin, place):
+            jnp.concatenate(chosen, axis=0),
+            right[origin, place, :, part * half:(part + 1) * half],
+            preferred_element_type=jnp.float32,
+        )
+        total[:, :, part * half:(part + 1) * half] += term.reshape(slots, side, half)
+
+    def cube_term(origin, place, part):
         label = left_labels[origin, 0, place]
         inner = origin * block_cols + lax.rem(label, block_cols)
         band = inner // block_rows
-        piece = squares[origin, place]
+        piece = squares[origin, place, :, part * half:(part + 1) * half]
         for slot, (own_row, own_col, out_row, out_col, live) in enumerate(owns):
             spot, found = find(right_labels, band, lax.rem(inner, block_rows) * block_cols + own_col)
             use = live & found & (label // block_cols == own_row)
             use = use & (mask[out_row, inner] > 0) & (mask[inner, out_col] > 0)
-            tile = right[band, spot]
+            tile = right[band, spot, part * half:(part + 1) * half, :]
             total[slot] += jnp.dot(
                 piece, jnp.where(use, tile, jnp.zeros_like(tile)), preferred_element_type=jnp.float32
             )
 
-    def stack_terms(origin, wait=None):
+    def stack_terms(origin, part, wait=None):
         for slot in range(slots):
             if wait is not None:
                 wait(slot)
-            square_term(origin, slot)
-
-    def mate_terms(at):
-        stack_terms(2 * at + 1 - lane, lambda slot: from_mate(slot + 1, at).wait_recv())
-
-    def consume(step):
+            square_term(origin, slot, part)
+
+    def mate_terms(at, part):
+        stack_terms(2 * at + 1 - lane, part, lambda slot: from_mate(slot + 1, at, part).wait_recv())
+
+    def consume(step, part):
         for way in range(2):
             @pl.when(arrives(way, step))
             def _():
                 heading = 1 if way == 0 else -1
-                stack_terms(2 * (place - heading * (step + 1)) + lane)
+                stack_terms(2 * (place - heading * (step + 1)) + lane, part)
         for way in range(2):
             @pl.when(arrives(way, step))
             def _():
                 heading = 1 if way == 0 else -1
-                mate_terms(place - heading * (step + 1))
+                mate_terms(place - heading * (step + 1), part)
+
+    def over(first, last, *bodies):
+        def body(step, unused):
+            for each in bodies:
+                each(step)
+            return unused
+
+        lax.fori_loop(first, last, body, 0)
+
+    def finish(part):
+        columns = slice(part * half, (part + 1) * half)
+        square[:, :, columns] = total[:, :, columns].astype(square.dtype)
+
+        def keep(slot):
+            squares[col, slot, :, columns] = square[slot, :, columns]
+
+        over(0, slots, keep)
+        gather = ColGather(
+            row, col, col_size, slots, square, squares, square_sems, part, part * half, half
+        )
+        gather.start()
+        return gather
 
     total[...] = jnp.zeros_like(total)
     for step in range(1, row_size):
@@ -314,57 +348,69 @@
         copy.start()
     for copy in copies:
         copy.wait()
-    turn(0, 0)
+    second = min(2, length - 1)
+    for step in range(second):
+        turn(step, 0)
     left_gather.forward()
     left_gather.collect(None, range(left_gather.chips))
-    stack_terms(row)
-    mate_terms(place)
-
-    def advance(step, unused):
-        turn(step, 0)
-        consume(step - 1)
-        return unused
-
-    lax.fori_loop(1, length - 1, advance, 0)
-    consume(length - 2)
-
-    square[...] = total[...].astype(square.dtype)
-
-    def keep(slot, unused):
-        squares[col, slot] = square[slot]
-        return unused
-
-    lax.fori_loop(0, slots, keep, 0)
-    square_gather = ColGather(row, col, col_size, slots, square, squares, square_sems)
-    square_gather.start()
+    stack_terms(row, 0)
+    mate_terms(place, 0)
+    over(second, length - 1, lambda step: turn(step, 0))
+    begin(1)
+    begin_mate(1)
+    over(0, length - 2, lambda step: consume(step, 0))
+    turn(0, 1)
+    consume(length - 2, 0)
+    first_gather = finish(0)
+    stack_terms(row, 1)
+    mate_terms(place, 1)
+    over(1, length - 1, lambda step: turn(step, 1), lambda step: consume(step - 1, 1))
+    first_gather.forward()
+    consume(length - 2, 1)
+    second_gather = finish(1)
+
     total[...] = jnp.zeros_like(total)
+
+    def first_term(origin, slot):
+        cube_term(origin, slot, 0)
+
+    def second_term(origin, slot):
+        cube_term(origin, slot, 1)
+
     for slot in range(slots):
-        cube_term(col, slot)
-    square_gather.collect(cube_term, [0])
-    square_gather.forward(cube_term)
-    square_gather.collect(cube_term, range(1, square_gather.chips))
+        first_term(col, slot)
+    for step in range(1, first_gather.chips):
+        for slot in range(slots):
+            first_term(first_gather.origin(step, first_gather.core), slot)
+    first_gather.collect(first_term, range(first_gather.chips))
+    for slot in range(slots):
+        second_term(col, slot)
+    second_gather.collect(second_term, [0])
+    second_gather.forward(second_term)
+    second_gather.collect(second_term, range(1, second_gather.chips))
     out[...] = (3.0 * square[...].astype(jnp.float32) - 2.0 * total[...]).astype(out.dtype)
 
     left_gather.settle()
-    square_gather.settle()
-
-    def settle(step, unused):
-        for index in range(count + 1):
-            for way in range(2):
-                @pl.when(goes(way, step))
-                def _():
-                    along(way, step, index).wait_send()
-        return unused
-
-    lax.fori_loop(0, length - 1, settle, 0)
-    own_to_mate(0).wait_send()
-
-    def collect(at, unused):
-        for index in range(1, count):
-            to_mate(index, at).wait_send()
-        return unused
-
-    lax.fori_loop(0, length, collect, 0)
+    first_gather.settle()
+    second_gather.settle()
+
+    def settle(step):
+        for part in range(2):
+            for index in range(count + 1):
+                for way in range(2):
+                    @pl.when(goes(way, step))
+                    def _():
+                        along(way, step, index, part).wait_send()
+
+    def collect(at):
+        for part in range(2):
+            for index in range(1, count):
+                to_mate(index, at, part).wait_send()
+
+    over(0, length - 1, settle)
+    over(0, length, collect)
+    for part in range(2):
+        own_to_mate(0, part).wait_send()
 
 
 def solution(mesh):
@@ -393,9 +439,9 @@
                 pltpu.SMEM((col_size, 8, 128), jnp.int32),
                 pltpu.SMEM((row_size, 8, 128), jnp.int32),
                 dma((4, chips, slots)),
-                dma((4, chips, slots)),
-                dma((2, 2, length, slots + 2)),
-                dma((2, length, slots + 1)),
+                dma((8, chips, slots)),
+                dma((4, 2, length, slots + 2)),
+                dma((4, length, slots + 1)),
                 dma((2, row_size)),
                 dma((2, col_size)),
                 dma((2,)),

time: 56.8 us -> 62.2 us (1.095)
  Pallas kernels: 54.8 us -> 60.2 us
    pallas_call x1, Pallas kernels: 54.8 us -> 60.2 us  [local(): pl.pallas_call(functools.partial(kernel, row_size, col_size), out_shape=j...]
where the time goes in v3:
time: 62.2 us; the launch traced here: 62 us
  Pallas kernels  60.2 us (97%)
  local copies, waits for them, and re-layouts  1.77 us (3%)
    pallas_call x1, Pallas kernels, local(): pl.pallas_call(functools.partial(kernel, row_size, col_size), out_shape=j...  60.2 us
    unnamed x1, local copies, waits for them, and re-layouts  1.77 us

profile of v3, /device:TPU:1, one launch (start us, length us, event | category | flops | bytes accessed | tf_op | source)
XLA Modules:
  0.0 62.0 jit_solution(14580244732548887602)
XLA Ops:
  0.0 60.2 %purify.1 = bf16[3,256,256]{2,1,0:T(8,128)(2,1)} custom-call(bf16[3,256,256]{2,1,0:T(8,128)(2,1)} %bitcast.4, s32[1,3]{1,0:T(1,128)} %bitcast.5, s32[64,64]{1,0:T(8,128)} %mask.1), custom_call_target="tpu_custom_call" | custom-call | tf_op jit(solution)/shard_map/purify/pallas_call | solution.py:425
  60.2 1.8 %copy.5 = bf16[1,1,3,256,256]{4,3,2,1,0:T(8,128)(2,1)} copy(bf16[1,1,3,256,256]{4,3,2,1,0:T(8,128)(2,1)} %bitcast.3) | data formatting | bytes 786432

commit v4 on v2

--- a/solution.py
+++ b/solution.py
@@ -112,8 +112,9 @@
     greet(row_size, col_size, row, col, True)
 
     pieces = [(slot, 0, side, False) for slot in range(slots - 1)]
-    pieces += [(slots - 1, half, half, False)]
-    early = (slots - 1, 0, half, True)
+    cut = side * 64 // 256
+    pieces += [(slots - 1, cut, side - cut, False)]
+    early = (slots - 1, 0, cut, True)
     mine = [early] + pieces
     count = len(mine)
 
@@ -178,6 +179,23 @@
         if way == 0:
             return (place - step >= 0) & (place + 1 < length)
         return (place + step < length) & (place > 0)
+
+    def id_row(step):
+        return send(
+            ids_out, right_ids.at[row], row_id_sems.at[0, step], row_id_sems.at[1, step],
+            lax.rem(row + step, row_size), col,
+        )
+
+    def id_col(step):
+        return send(
+            ids_out, left_ids.at[col], col_id_sems.at[0, step], col_id_sems.at[1, step],
+            row, lax.rem(col + step, col_size),
+        )
+
+    for step in range(1, row_size):
+        id_row(step).start()
+    for step in range(1, col_size):
+        id_col(step).start()
 
     own_to_mate(0).start()
     for index in range(count):
@@ -190,22 +208,6 @@
     left_gather = ColGather(row, col, col_size, slots, tiles, left, col_sems)
     left_gather.start()
 
-    def id_row(step):
-        return send(
-            ids_out, right_ids.at[row], row_id_sems.at[0, step], row_id_sems.at[1, step],
-            lax.rem(row + step, row_size), col,
-        )
-
-    def id_col(step):
-        return send(
-            ids_out, left_ids.at[col], col_id_sems.at[0, step], col_id_sems.at[1, step],
-            row, lax.rem(col + step, col_size),
-        )
-
-    for step in range(1, row_size):
-        id_row(step).start()
-    for step in range(1, col_size):
-        id_col(step).start()
 
     from_mate(0, place).wait_recv()
     for way in range(2):
@@ -302,6 +304,7 @@
                 mate_terms(place - heading * (step + 1))
 
     total[...] = jnp.zeros_like(total)
+    turn(0, 0)
     for step in range(1, row_size):
         id_row(step).wait()
     for step in range(1, col_size):
@@ -314,7 +317,6 @@
         copy.start()
     for copy in copies:
         copy.wait()
-    turn(0, 0)
     left_gather.forward()
     left_gather.collect(None, range(left_gather.chips))
     stack_terms(row)

time: 56.8 us -> 56.3 us (level)
  no operation moved by 1% of the time
where the time goes in v4:
time: 56.3 us; the launch traced here: 56.1 us
  Pallas kernels  54.3 us (96%)
  local copies, waits for them, and re-layouts  1.77 us (3%)
    pallas_call x1, Pallas kernels, local(): pl.pallas_call(functools.partial(kernel, row_size, col_size), out_shape=j...  54.3 us
    unnamed x1, local copies, waits for them, and re-layouts  1.77 us

profile of v4, /device:TPU:1, one launch (start us, length us, event | category | flops | bytes accessed | tf_op | source)
XLA Modules:
  0.0 56.1 jit_solution(18257709229323432254)
XLA Ops:
  0.0 54.3 %purify.1 = bf16[3,256,256]{2,1,0:T(8,128)(2,1)} custom-call(bf16[3,256,256]{2,1,0:T(8,128)(2,1)} %bitcast.4, s32[1,3]{1,0:T(1,128)} %bitcast.5, s32[64,64]{1,0:T(8,128)} %mask.1), custom_call_target="tpu_custom_call" | custom-call | tf_op jit(solution)/shard_map/purify/pallas_call | solution.py:381
  54.3 1.8 %copy.5 = bf16[1,1,3,256,256]{4,3,2,1,0:T(8,128)(2,1)} copy(bf16[1,1,3,256,256]{4,3,2,1,0:T(8,128)(2,1)} %bitcast.3) | data formatting | bytes 786432

commit v5 on v4

--- a/solution.py
+++ b/solution.py
@@ -197,6 +197,8 @@
     for step in range(1, col_size):
         id_col(step).start()
 
+    left_gather = ColGather(row, col, col_size, slots, tiles, left, col_sems)
+    left_gather.start()
     own_to_mate(0).start()
     for index in range(count):
         for way in range(2):
@@ -205,8 +207,6 @@
                 along(way, 0, index, True).start()
         if index:
             own_to_mate(index).start()
-    left_gather = ColGather(row, col, col_size, slots, tiles, left, col_sems)
-    left_gather.start()
 
 
     from_mate(0, place).wait_recv()
@@ -332,13 +332,16 @@
 
     square[...] = total[...].astype(square.dtype)
 
+    square_gather = ColGather(row, col, col_size, slots, square, squares, square_sems)
+
     def keep(slot, unused):
         squares[col, slot] = square[slot]
+        for step in range(1, square_gather.chips):
+            square_gather.across(step, slot).start()
+        square_gather.beside(0, slot).start()
         return unused
 
     lax.fori_loop(0, slots, keep, 0)
-    square_gather = ColGather(row, col, col_size, slots, square, squares, square_sems)
-    square_gather.start()
     total[...] = jnp.zeros_like(total)
     for slot in range(slots):
         cube_term(col, slot)

time: 56.3 us -> 56.2 us (level)
  no operation moved by 1% of the time
where the time goes in v5:
time: 56.2 us; the launch traced here: 56 us
  Pallas kernels  54.3 us (97%)
  local copies, waits for them, and re-layouts  1.77 us (3%)
    pallas_call x1, Pallas kernels, local(): pl.pallas_call(functools.partial(kernel, row_size, col_size), out_shape=j...  54.3 us
    unnamed x1, local copies, waits for them, and re-layouts  1.77 us

profile of v5, /device:TPU:1, one launch (start us, length us, event | category | flops | bytes accessed | tf_op | source)
XLA Modules:
  0.0 56.0 jit_solution(4714833451662923179)
XLA Ops:
  0.0 54.3 %purify.1 = bf16[3,256,256]{2,1,0:T(8,128)(2,1)} custom-call(bf16[3,256,256]{2,1,0:T(8,128)(2,1)} %bitcast.4, s32[1,3]{1,0:T(1,128)} %bitcast.5, s32[64,64]{1,0:T(8,128)} %mask.1), custom_call_target="tpu_custom_call" | custom-call | tf_op jit(solution)/shard_map/purify/pallas_call | solution.py:384
  54.3 1.8 %copy.5 = bf16[1,1,3,256,256]{4,3,2,1,0:T(8,128)(2,1)} copy(bf16[1,1,3,256,256]{4,3,2,1,0:T(8,128)(2,1)} %bitcast.3) | data formatting | bytes 786432
